TPU v7x, 32 devices: a whole 2x2x4 slice. The times are simulated.
32 devices in a mesh: seq: 32 (over z, y, x, core).
Axes of the slice: x: 2, y: 2, z: 4, core: 2. Of those that a mesh axis runs over, the one named last changes fastest.
Arguments:
- queries: bfloat16 [8192, 8, 128], P('seq'), may hold values from -132 to 132
- keys: bfloat16 [16384, 8, 128], P('seq'), may hold values from -6 to 6
- values: bfloat16 [16384, 8, 128], P('seq'), may hold values from -6 to 6
- routes: int32 [8192, 8], P('seq'), may hold values from 0 to 63, all different within a row; in each aligned block of 256 rows (0 to 255, 256 to 511, ...) at most 40 rows name the same one
Outputs:
- attended: bfloat16 [8192, 8, 128], P('seq')
Inputs may be any that keep to these rules, and one draw needn't show every extreme that they name: `routes`: each row names 8 different heads; among the 256 rows of one device no head is named more than 40 times, a bound that some block reaches.
All inputs are finite; a program needn't handle non-finite values.
Results may differ from a plain program's by a relative error of at most 0.0065.
Values may be sent and summed in bfloat16 or wider, within the bound.
A program may use at most 64 MiB of HBM per device.

v0:
```python
import functools
import math

import jax
import jax.numpy as jnp
from jax import lax
from jax.experimental import pallas as pl
from jax.experimental.pallas import tpu as pltpu
from jax.sharding import PartitionSpec as P

HEADS = 64
HOPS = 4
MOST = 40
LANES = 128
LOW = -1e30
MESH = pl.DeviceIdType.MESH


def dot(a, b):
    return lax.dot_general(a, b, (((1,), (0,)), ((), ())), preferred_element_type=jnp.float32)


def dot_t(a, b):
    return lax.dot_general(a, b, (((1,), (1,)), ((), ())), preferred_element_type=jnp.float32)


def pack_kernel(groups, capacity, q_ref, routes_ref, packed_ref, pos_ref, slots_ref, wide):
    tokens, routed, width = q_ref.shape
    per_group = HEADS // groups
    wide[...] = q_ref[...].astype(jnp.float32)
    lane = lax.broadcasted_iota(jnp.int32, (tokens, LANES), 1)
    turned = routes_ref[...].astype(jnp.float32)
    group_of = jnp.concatenate([turned] * (LANES // routed), axis=0).T.astype(jnp.int32) // per_group
    hots = [(group_of[:, r : r + 1] == lane).astype(jnp.float32) for r in range(routed)]
    count = functools.reduce(jnp.add, hots)
    row = lax.broadcasted_iota(jnp.int32, (tokens, tokens), 0)
    col = lax.broadcasted_iota(jnp.int32, (tokens, tokens), 1)
    lower = (col < row).astype(jnp.bfloat16)
    rank = dot(lower, count.astype(jnp.bfloat16)) + (lane * capacity).astype(jnp.float32)
    slots = jnp.zeros((tokens, LANES), jnp.float32)
    for r in range(routed):
        slot = jnp.sum(hots[r] * rank, axis=1, keepdims=True)
        slots = jnp.where(lane == r, slot, slots)
        rank = rank + hots[r]
    slots_ref[...] = slots.astype(jnp.int32)
    slots_t = slots.T.astype(jnp.int32)
    token = lax.broadcasted_iota(jnp.int32, (tokens, width), 0).astype(jnp.bfloat16)
    rights = [
        jnp.concatenate([wide[:, r, :].astype(jnp.bfloat16), token], axis=1) for r in range(routed)
    ]
    step = 256
    total = groups * capacity
    place = lax.broadcasted_iota(jnp.int32, (step, tokens), 0)
    for at in range(0, total, step):
        acc = jnp.zeros((step, 2 * width), jnp.float32)
        for r in range(routed):
            here = (place == slots_t[r : r + 1, :] - at).astype(jnp.float32).astype(jnp.bfloat16)
            acc = acc + dot(here, rights[r])
        packed_ref[pl.ds(at, step), :] = acc[:, :width].astype(jnp.bfloat16)
        pos_ref[pl.ds(at, step), :] = acc[:, width:]


def unpack_kernel(fin_ref, slots_ref, out_ref, wide):
    tokens, routed, width = out_ref.shape
    total = fin_ref.shape[0]
    lane = lax.broadcasted_iota(jnp.int32, (tokens, 256), 1)
    for r in range(routed):
        slot = slots_ref[:, r : r + 1]
        acc = jnp.zeros((tokens, width), jnp.float32)
        for at in range(0, total, 256):
            here = (lane == slot - at).astype(jnp.float32).astype(jnp.bfloat16)
            acc = acc + dot(here, fin_ref[pl.ds(at, 256), :])
        wide[:, r, :] = acc
    out_ref[...] = wide[...].astype(jnp.bfloat16)


def remote(src, dst, send, recv, device):
    return pltpu.make_async_remote_copy(
        src_ref=src, dst_ref=dst, send_sem=send, recv_sem=recv,
        device_id=(device,), device_id_type=MESH,
    )


def attend(q, k, v, scale, mask=None):
    s = dot_t(q, k) * scale
    if mask is not None:
        s = mask(s)
    top = jnp.max(s, axis=1, keepdims=True)
    p = jnp.exp2(s - top).astype(jnp.bfloat16)
    ones = jnp.ones(v.shape, jnp.bfloat16)
    both = dot(p, jnp.concatenate([v, ones], axis=1))
    width = v.shape[1]
    total = both[:, width:]
    return both[:, :width] / total, top + jnp.log2(total)


def squeeze(lse, padded):
    rows = lse.shape[0]
    return jnp.concatenate([lse, jnp.zeros((padded - rows, LANES), jnp.float32)], axis=0).T[:8]


def widen(tile, rows):
    return jnp.concatenate([tile] * (LANES // 8), axis=0).T[:rows]


def merge(parts):
    top = functools.reduce(jnp.maximum, [lse for _, lse in parts])
    weights = [jnp.exp2(lse - top) for _, lse in parts]
    total = functools.reduce(jnp.add, weights)
    mixed = functools.reduce(jnp.add, [o.astype(jnp.float32) * w for (o, _), w in zip(parts, weights)])
    return mixed / total, top + jnp.log2(total)


def main_kernel(
    n, q, pos, k8, v8, fin, kh, vh, qb, qc, qd, oa, la, ob, lb, tb, rb, sb,
    oc, tc, od, ld, td, rx, sx, rc, sc, rd, sd,
    kv_send, kv_recv, kv_local, qb_sem, qc_send, qc_recv, qd_send, qd_recv, relay_send,
    ob_send, ob_recv, tb_send, tb_recv, oc_send, tc_send, od_send, td_send,
    rx_recv, sx_recv, rc_recv, sc_recv, rd_recv, sd_recv,
):
    groups, capacity, width = q.shape
    context = k8.shape[1]
    tokens = context // 2
    padded = tb.shape[2]
    half = groups // 2
    chips = n // 2
    me = lax.axis_index("seq")
    c = me // 2
    k = me % 2
    other = 1 - k
    partner = c * 2 + other
    even = c % 2 == 0
    odd = c % 2 == 1
    scale = jnp.float32(math.log2(math.e) / math.sqrt(width))
    exists = {-2: c >= 2, -1: c >= 1, 1: c + 1 < chips, 2: c + 2 < chips}
    near = jnp.logical_and(odd, exists[-1])

    barrier = pltpu.get_barrier_semaphore()

    def signal(device):
        pl.semaphore_signal(barrier, inc=1, device_id=(device,), device_id_type=MESH)

    signal(partner)
    peers = 1
    for far, there in exists.items():
        @pl.when(there)
        def _(far=far):
            signal((c + far) * 2)
            signal((c + far) * 2 + 1)
        peers = peers + 2 * there.astype(jnp.int32)
    pl.semaphore_wait(barrier, peers)

    def query_copy(x, s, r, far, g8):
        j, g = g8 // half, g8 % half
        return remote(q.at[g8], x.at[k, g], s.at[g8], r.at[k, g], (c - far) * 2 + j)

    for g8 in [j * half + g for g in range(half) for j in range(2)]:
        @pl.when(exists[-2])
        def _(g8=g8):
            query_copy(qd, qd_send, qd_recv, 2, g8).start()
        @pl.when(near)
        def _(g8=g8):
            query_copy(qc, qc_send, qc_recv, 1, g8).start()

    def kv_copies():
        return [
            remote(a.at[pl.ds(other * half, half)], b.at[k], kv_send.at[i], kv_recv.at[i], partner)
            for i, (a, b) in enumerate(((k8, kh), (v8, vh)))
        ]

    def kv_locals():
        return [
            pltpu.make_async_copy(a.at[pl.ds(k * half, half)], b.at[k], kv_local.at[i])
            for i, (a, b) in enumerate(((k8, kh), (v8, vh)))
        ]

    for one in kv_copies() + kv_locals():
        one.start()

    def qb_copy():
        return remote(q.at[pl.ds(0, half)], qb, qb_sem.at[0], qb_sem.at[1], partner)

    @pl.when(k == 1)
    def _():
        qb_copy().start()

    column = lax.broadcasted_iota(jnp.int32, (capacity, tokens), 1).astype(jnp.float32)

    def own(g, carry):
        limit = jnp.concatenate([pos[g]] * (tokens // LANES), axis=1)

        def mask(s):
            tail = jnp.where(column <= limit, s[:, context - tokens :], jnp.float32(LOW))
            return jnp.concatenate([s[:, : context - tokens], tail], axis=1)

        oa[g], la[g] = attend(q[g], k8[g], v8[g], scale, mask)
        return carry

    lax.fori_loop(0, groups, own, 0)

    for one in kv_copies():
        one.wait_recv()
    for one in kv_locals():
        one.wait()

    @pl.when(k == 0)
    def _():
        qb_copy().wait_recv()

    def b_copies(g):
        return (
            remote(ob.at[g], rb.at[g], ob_send.at[g], ob_recv.at[g], partner),
            remote(tb.at[g], sb.at[g], tb_send.at[g], tb_recv.at[g], partner),
        )

    def c_near(j, g):
        at = k * half + g
        to = (c + 1) * 2 + j
        return (
            remote(oc.at[j, g], rc.at[at], oc_send.at[j, g], rc_recv.at[at], to),
            remote(tc.at[j, g], sc.at[at], tc_send.at[j, g], sc_recv.at[at], to),
        )

    def c_relay(j, g):
        to = (c - 1) * 2 + k
        return (
            remote(oc.at[j, g], rx.at[j, g], oc_send.at[j, g], rx_recv.at[j, g], to),
            remote(tc.at[j, g], sx.at[j, g], tc_send.at[j, g], sx_recv.at[j, g], to),
        )

    def d_copies(j, g):
        at = k * half + g
        to = (c + 2) * 2 + j
        return (
            remote(od.at[j, g], rd.at[at], od_send.at[j, g], rd_recv.at[at], to),
            remote(td.at[j, g], sd.at[at], td_send.at[j, g], sd_recv.at[at], to),
        )

    def query_relay(j, g):
        return remote(
            qd.at[j, g], qc.at[j, g], relay_send.at[j, g], qc_recv.at[j, g], (c + 1) * 2 + k
        )

    def start(copies):
        for one in copies:
            one.start()

    def both(x, g):
        return jnp.concatenate([x[0, g], x[1, g]], axis=0)

    lag, delay = 1, 3

    def step(i, carry):
        @pl.when(jnp.logical_and(i < groups, exists[2]))
        def _():
            g, j = i // 2, i % 2
            remote(qd.at[j, g], qd.at[j, g], qd_send.at[0], qd_recv.at[j, g], partner).wait_recv()

            @pl.when(even)
            def _():
                query_relay(j, g).start()

            def put(out, lse):
                od[j, g] = out.astype(jnp.bfloat16)
                ld[j, g] = lse

            @pl.when(j == 0)
            def _():
                put(*attend(qd[j, g], both(kh, g), both(vh, g), scale))

            @pl.when(j == 1)
            def _():
                put(*attend(qd[j, g], kh[1, g], vh[1, g], scale))

            @pl.when(odd)
            def _():
                td[j, g] = squeeze(ld[j, g], padded)
                start(d_copies(j, g))

        @pl.when(i < half)
        def _():
            @pl.when(k == 1)
            def _():
                qb[i] = q[half + i]

            out, lse = attend(qb[i], kh[0, i], vh[0, i], scale)
            ob[i] = out.astype(jnp.bfloat16)
            lb[i] = lse

            @pl.when(k == 0)
            def _():
                tb[i] = squeeze(lse, padded)
                start(b_copies(i))

        @pl.when(jnp.logical_and(jnp.logical_and(i >= lag, i < groups + lag), exists[1]))
        def _():
            at = i - lag
            g, j = at // 2, at % 2
            remote(qc.at[j, g], qc.at[j, g], qc_send.at[0], qc_recv.at[j, g], partner).wait_recv()
            out, lse = attend(qc[j, g], both(kh, g), both(vh, g), scale)
            oc[j, g] = out.astype(jnp.bfloat16)
            tc[j, g] = squeeze(lse, padded)

            @pl.when(even)
            def _():
                start(c_near(j, g))

            @pl.when(odd)
            def _():
                start(c_relay(j, g))

        @pl.when(jnp.logical_and(jnp.logical_and(i >= delay, even), exists[2]))
        def _():
            at = i - delay
            g, j = at // 2, at % 2
            remote(oc.at[j, g], rx.at[j, g], oc_send.at[j, g], rx_recv.at[j, g], partner).wait_recv()
            remote(tc.at[j, g], sx.at[j, g], tc_send.at[j, g], sx_recv.at[j, g], partner).wait_recv()
            out, lse = merge([(od[j, g], ld[j, g]), (rx[j, g], widen(sx[j, g], capacity))])
            od[j, g] = out.astype(jnp.bfloat16)
            td[j, g] = squeeze(lse, padded)
            start(d_copies(j, g))

        return carry

    lax.fori_loop(0, groups + delay, step, 0)

    def absent(o, t):
        o[...] = jnp.zeros(o.shape, o.dtype)
        t[...] = jnp.full(t.shape, LOW, t.dtype)

    @pl.when(jnp.logical_not(near))
    def _():
        absent(rc, sc)

    @pl.when(jnp.logical_not(exists[-2]))
    def _():
        absent(rd, sd)

    @pl.when(k == 0)
    def _():
        absent(rb, sb)

    def finish(g8, carry):
        @pl.when(near)
        def _():
            remote(oc.at[0, 0], rc.at[g8], oc_send.at[0, 0], rc_recv.at[g8], partner).wait_recv()
            remote(tc.at[0, 0], sc.at[g8], tc_send.at[0, 0], sc_recv.at[g8], partner).wait_recv()

        @pl.when(exists[-2])
        def _():
            remote(od.at[0, 0], rd.at[g8], od_send.at[0, 0], rd_recv.at[g8], partner).wait_recv()
            remote(td.at[0, 0], sd.at[g8], td_send.at[0, 0], sd_recv.at[g8], partner).wait_recv()

        parts = [
            (oa[g8], la[g8]), (rc[g8], widen(sc[g8], capacity)), (rd[g8], widen(sd[g8], capacity))
        ]
        second = jnp.logical_and(k == 1, g8 < half)

        @pl.when(second)
        def _():
            for one in b_copies(g8 % half):
                one.wait_recv()
            g = g8 % half
            fin[g8] = merge(parts + [(rb[g], widen(sb[g], capacity))])[0].astype(jnp.bfloat16)

        @pl.when(jnp.logical_not(second))
        def _():
            g = g8 % half
            lse = jnp.where(k == 1, lb[g], jnp.float32(LOW))
            fin[g8] = merge(parts + [(ob[g], lse)])[0].astype(jnp.bfloat16)

        return carry

    lax.fori_loop(0, groups, finish, 0)

    for one in kv_copies():
        one.wait_send()

    @pl.when(k == 1)
    def _():
        qb_copy().wait_send()

    def sent(there, make):
        @pl.when(there)
        def _():
            for j in range(2):
                for g in range(half):
                    for one in make(j, g):
                        one.wait_send()

    @pl.when(k == 0)
    def _():
        for g in range(half):
            for one in b_copies(g):
                one.wait_send()

    sent(exists[-2], lambda j, g: (query_copy(qd, qd_send, qd_recv, 2, j * half + g),))
    sent(near, lambda j, g: (query_copy(qc, qc_send, qc_recv, 1, j * half + g),))
    sent(jnp.logical_and(even, exists[2]), lambda j, g: (query_relay(j, g),))
    sent(exists[2], d_copies)
    sent(jnp.logical_and(even, exists[1]), c_near)
    sent(jnp.logical_and(odd, exists[1]), c_relay)


def shards(n, queries, keys, values, routes):
    tokens, routed, width = queries.shape
    context, groups, _ = keys.shape
    capacity = HEADS // groups * MOST
    half = groups // 2
    padded = -(-capacity // LANES) * LANES
    total = groups * capacity
    vmem = pl.BlockSpec(memory_space=pltpu.VMEM)
    packed, pos, slots = pl.pallas_call(
        functools.partial(pack_kernel, groups, capacity),
        out_shape=(
            jax.ShapeDtypeStruct((total, width), jnp.bfloat16),
            jax.ShapeDtypeStruct((total, width), jnp.float32),
            jax.ShapeDtypeStruct((tokens, LANES), jnp.int32),
        ),
        in_specs=[vmem] * 2,
        out_specs=(vmem,) * 3,
        scratch_shapes=[pltpu.VMEM((tokens, routed, width), jnp.float32)],
        name="pack",
    )(queries, routes.T)
    k8 = keys.transpose(1, 0, 2)
    v8 = values.transpose(1, 0, 2)
    bf = lambda *shape: pltpu.VMEM(shape, jnp.bfloat16)
    f32 = lambda *shape: pltpu.VMEM(shape, jnp.float32)
    sem = lambda *shape: pltpu.SemaphoreType.DMA(shape)
    chunks = lambda: bf(2, half, capacity, width)
    fin = pl.pallas_call(
        functools.partial(main_kernel, n),
        out_shape=jax.ShapeDtypeStruct((groups, capacity, width), jnp.bfloat16),
        in_specs=[vmem] * 4,
        out_specs=vmem,
        scratch_shapes=[
            bf(2, half, context, width), bf(2, half, context, width),
            bf(half, capacity, width), chunks(), chunks(),
            f32(groups, capacity, width), f32(groups, capacity, width),
            bf(half, capacity, width), f32(half, capacity, width), f32(half, 8, padded),
            bf(half, capacity, width), f32(half, 8, padded),
            chunks(), f32(2, half, 8, padded),
            chunks(), f32(2, half, capacity, width), f32(2, half, 8, padded),
            chunks(), f32(2, half, 8, padded),
            bf(groups, capacity, width), f32(groups, 8, padded),
            bf(groups, capacity, width), f32(groups, 8, padded),
            sem(2), sem(2), sem(2), sem(2),
            sem(groups), sem(2, half), sem(groups), sem(2, half), sem(2, half),
            sem(half), sem(half), sem(half), sem(half),
            sem(2, half), sem(2, half), sem(2, half), sem(2, half),
            sem(2, half), sem(2, half), sem(groups), sem(groups), sem(groups), sem(groups),
        ],
        compiler_params=pltpu.CompilerParams(
            collective_id=0, has_side_effects=True, vmem_limit_bytes=60 * 1024 * 1024
        ),
        name="main",
    )(packed.reshape(groups, capacity, width), pos.reshape(groups, capacity, width), k8, v8)
    return pl.pallas_call(
        unpack_kernel,
        out_shape=jax.ShapeDtypeStruct((tokens, routed, width), jnp.bfloat16),
        in_specs=[vmem] * 2,
        out_specs=vmem,
        scratch_shapes=[pltpu.VMEM((tokens, routed, width), jnp.float32)],
        name="unpack",
    )(fin.reshape(total, width), slots)


def solution(mesh):
    n = mesh.shape["seq"]
    placed = (P("seq", None, None), P("seq", None, None), P("seq", None, None), P("seq", None))
    return jax.shard_map(
        functools.partial(shards, n),
        mesh=mesh,
        in_specs=placed,
        out_specs=P("seq", None, None),
        check_vma=False,
    )
```

profile of v0, /device:TPU:21, one launch (start us, length us, event | category | flops | bytes accessed | tf_op | source)
XLA Modules:
  0.0 67.8 jit_solution(12032181981176756883)
XLA Ops:
  0.0 7.0 %pack.1 = (bf16[2560,128]{1,0:T(8,128)(2,1)}, f32[2560,128]{1,0:T(8,128)}, s32[256,128]{1,0:T(8,128)}) custom-call(bf16[256,8,128]{2,1,0:T(8,128)(2,1)} %q_ref.1, s32[8,256]{1,0:T(8,128)} %bitcast.11), custom_call_target="tpu_custom_call" | custom-call | tf_op jit(solution)/shard_map/pack/pallas_call | solution.py:413
  7.0 3.2 %copy_bitcast_fusion = (bf16[8,512,128]{2,1,0:T(8,128)(2,1)}, bf16[8,512,128]{2,1,0:T(8,128)(2,1)}) fusion(bf16[512,8,128]{2,1,0:T(8,128)(2,1)} %param.6, bf16[512,8,128]{2,1,0:T(8,128)(2,1)} %param.5), kind=kLoop, calls=%fused_computation | loop fusion | bytes 4194304 | tf_op jit(solution)/shard_map/transpose | solution.py:426
  10.3 52.2 %main.1 = bf16[8,320,128]{2,1,0:T(8,128)(2,1)} custom-call(bf16[8,320,128]{2,1,0:T(8,128)(2,1)} %bitcast.10, f32[8,320,128]{2,1,0:T(8,128)} %bitcast.9, bf16[8,512,128]{2,1,0:T(8,128)(2,1)} %get-tuple-element.12.k8, bf16[8,512,128]{2,1,0:T(8,128)(2,1)} %get-tuple-element.11.v8), custom_call_target="tpu_custom_call" | custom-call | tf_op jit(solution)/shard_map/main/pallas_call | solution.py:431
  62.5 5.4 %unpack.1 = bf16[256,8,128]{2,1,0:T(8,128)(2,1)} custom-call(bf16[2560,128]{1,0:T(8,128)(2,1)} %bitcast.8, s32[256,128]{1,0:T(8,128)} %get-tuple-element.10.slots_ref), custom_call_target="tpu_custom_call" | custom-call | tf_op jit(solution)/shard_map/unpack/pallas_call | solution.py:458
where the time goes:
time: 68 us; the launch traced here: 67.8 us
  Pallas kernels  64.6 us (95%)
  local copies, waits for them, and re-layouts  3.23 us (5%)
    pallas_call x1, Pallas kernels, shards(): pl.pallas_call(functools.partial(main_kernel, n), out_shape=jax.ShapeDtyp...  52.2 us
    pallas_call x1, Pallas kernels, shards(): pl.pallas_call(functools.partial(pack_kernel, groups, capacity), out_shap...  7.04 us
    pallas_call x1, Pallas kernels, shards(): pl.pallas_call(unpack_kernel, out_shape=jax.ShapeDtypeStruct((tokens, rou...  5.36 us
    transpose x1, local copies, waits for them, and re-layouts, shards(): v8 = values.transpose(1, 0, 2)  3.23 us

commit v1 on v0

v1 whole, which is shorter than its diff:
```python
import functools
import math

import jax
import jax.numpy as jnp
from jax import lax
from jax.experimental import pallas as pl
from jax.experimental.pallas import tpu as pltpu
from jax.sharding import PartitionSpec as P

HEADS = 64
MOST = 40
LANES = 128
LOW = -1e30
MESH = pl.DeviceIdType.MESH


def dot(a, b):
    return lax.dot_general(a, b, (((1,), (0,)), ((), ())), preferred_element_type=jnp.float32)


def dot_t(a, b):
    return lax.dot_general(a, b, (((1,), (1,)), ((), ())), preferred_element_type=jnp.float32)


def remote(src, dst, send, recv, device):
    return pltpu.make_async_remote_copy(
        src_ref=src, dst_ref=dst, send_sem=send, recv_sem=recv,
        device_id=(device,), device_id_type=MESH,
    )


def attend(q, k, v, scale, mask=None):
    s = dot_t(q, k) * scale
    if mask is not None:
        s = mask(s)
    top = jnp.max(s, axis=1, keepdims=True)
    p = jnp.exp2(s - top).astype(jnp.bfloat16)
    ones = jnp.ones(v.shape, jnp.bfloat16)
    both = dot(p, jnp.concatenate([v, ones], axis=1))
    width = v.shape[1]
    total = both[:, width:]
    return both[:, :width] / total, top + jnp.log2(total)


def squeeze(lse, padded):
    rows = lse.shape[0]
    return jnp.concatenate([lse, jnp.zeros((padded - rows, LANES), jnp.float32)], axis=0).T[:1]


def widen(row, rows):
    return jnp.concatenate([jnp.broadcast_to(row, (8, row.shape[1]))] * (LANES // 8), axis=0).T[:rows]


def merge(parts):
    top = functools.reduce(jnp.maximum, [lse for _, lse in parts])
    weights = [jnp.exp2(lse - top) for _, lse in parts]
    total = functools.reduce(jnp.add, weights)
    mixed = functools.reduce(jnp.add, [o.astype(jnp.float32) * w for (o, _), w in zip(parts, weights)])
    return mixed / total, top + jnp.log2(total)


def kernel(
    n, q_in, routes_t, k_hbm, v_hbm, out,
    raw, wide, rights, slot_rows, slots, q, pos, kall, vall,
    qc, qd, oa, la, oc, tc, od, ld, td, rx, sx, rc, sc, rd, sd, fin, acc,
    raw_sem, kv_send, kv_recv, qn_send, qd_send, qc_recv, qd_recv, relay_send,
    oc_send, tc_send, od_send, td_send,
    rx_recv, sx_recv, rc_recv, sc_recv, rd_recv, sd_recv,
):
    tokens, routed, width = q_in.shape
    groups, capacity, _ = q.shape
    context = kall.shape[2]
    padded = tc.shape[2]
    per_group = HEADS // groups
    chips = n // 2
    me = lax.axis_index("seq")
    c = me // 2
    k = me % 2
    partner = c * 2 + 1 - k
    even = c % 2 == 0
    odd = c % 2 == 1
    scale = jnp.float32(math.log2(math.e) / math.sqrt(width))
    below = c >= 2
    above = c + 2 < chips
    mate = jnp.where(even, c + 1, c - 1) * 2 + k
    feeds = jnp.logical_or(even, c + 1 < chips)
    down = (c - 2) * 2 + k
    up = (c + 2) * 2 + k

    barrier = pltpu.get_barrier_semaphore()

    def signal(device):
        pl.semaphore_signal(barrier, inc=1, device_id=(device,), device_id_type=MESH)

    signal(partner)
    signal(mate)

    @pl.when(below)
    def _():
        signal(down)

    @pl.when(above)
    def _():
        signal(up)

    raws = [pltpu.make_async_copy(a, raw.at[i], raw_sem.at[i]) for i, a in enumerate((k_hbm, v_hbm))]
    for one in raws:
        one.start()

    group_of = routes_t[...] // per_group
    group = lax.broadcasted_iota(jnp.int32, (groups, tokens), 0)
    hots = [(group_of[r : r + 1] == group).astype(jnp.float32) for r in range(routed)]
    count = functools.reduce(jnp.add, hots)
    row = lax.broadcasted_iota(jnp.int32, (tokens, tokens), 0)
    col = lax.broadcasted_iota(jnp.int32, (tokens, tokens), 1)
    upper = (row < col).astype(jnp.float32).astype(jnp.bfloat16)
    rank = dot(count.astype(jnp.bfloat16), upper) + (group * capacity).astype(jnp.float32)
    rows = []
    for r in range(routed):
        rows.append(jnp.sum(hots[r] * rank, axis=0, keepdims=True))
        rank = rank + hots[r]
    slot_all = jnp.concatenate(rows, axis=0)
    slot_rows[...] = slot_all
    slots[...] = jnp.concatenate([slot_all] * (LANES // routed), axis=0).T

    wide[pl.ds(0, tokens)] = q_in[...].astype(jnp.float32)
    token = lax.broadcasted_iota(jnp.int32, (tokens, width), 0).astype(jnp.float32).astype(jnp.bfloat16)
    for r in range(routed):
        rights[pl.ds(r * tokens, tokens), :width] = wide[pl.ds(0, tokens), r, :].astype(jnp.bfloat16)
        rights[pl.ds(r * tokens, tokens), width:] = token

    pl.semaphore_wait(barrier, 2 + below.astype(jnp.int32) + above.astype(jnp.int32))

    def query_down(g):
        return remote(q.at[g], qd.at[g], qd_send.at[g], qd_recv.at[g], down)

    def query_near(g):
        return remote(q.at[g], qc.at[g], qn_send.at[g], qc_recv.at[g], mate)

    place = lax.broadcasted_iota(jnp.int32, (capacity, tokens), 0).astype(jnp.float32)

    def pack(g, carry):
        at = (g * capacity).astype(jnp.float32)
        here = jnp.concatenate(
            [
                (place == slot_rows[r : r + 1] - at).astype(jnp.float32).astype(jnp.bfloat16)
                for r in range(routed)
            ],
            axis=1,
        )
        both = dot(here, rights[...])
        q[g] = both[:, :width].astype(jnp.bfloat16)
        pos[g] = both[:, width:]

        @pl.when(below)
        def _():
            query_down(g).start()

        @pl.when(odd)
        def _():
            query_near(g).start()

        return carry

    lax.fori_loop(0, groups, pack, 0)

    part = 128

    def turn(i, to):
        def body(s, carry):
            at = pl.multiple_of(s * part, part)
            wide[pl.ds(0, part)] = raw[i, pl.ds(at, part)].astype(jnp.float32)
            for g in range(groups):
                to[g, k, pl.ds(at, part), :] = wide[pl.ds(0, part), g, :].astype(jnp.bfloat16)
            return carry

        lax.fori_loop(0, context // part, body, 0)

    def kv_copy(i):
        a = (kall, vall)[i]
        return remote(a.at[:, k], a.at[:, k], kv_send.at[i], kv_recv.at[i], partner)

    def kv_arrival(i):
        a = (kall, vall)[i]
        return remote(a.at[:, 1 - k], a.at[:, 1 - k], kv_send.at[i], kv_recv.at[i], partner)

    for i, to in enumerate((kall, vall)):
        raws[i].wait()
        turn(i, to)
        kv_copy(i).start()
    for i in range(2):
        kv_arrival(i).wait_recv()

    column = lax.broadcasted_iota(jnp.int32, (capacity, tokens), 1).astype(jnp.float32)

    def all_of(a, g):
        return a[g].reshape(2 * context, width)

    def own(g, keys, values):
        limit = jnp.concatenate([pos[g]] * (tokens // LANES), axis=1)

        def mask(s):
            free = s.shape[1] - tokens
            tail = jnp.where(column <= limit, s[:, free:], jnp.float32(LOW))
            return jnp.concatenate([s[:, :free], tail], axis=1)

        oa[g], la[g] = attend(q[g], keys, values, scale, mask)

    def relay(g):
        return remote(qd.at[g], qc.at[g], relay_send.at[g], qc_recv.at[g], mate)

    def c_near(g):
        return (
            remote(oc.at[g], rc.at[g], oc_send.at[g], rc_recv.at[g], mate),
            remote(tc.at[g], sc.at[g], tc_send.at[g], sc_recv.at[g], mate),
        )

    def c_relay(g):
        return (
            remote(oc.at[g], rx.at[g], oc_send.at[g], rx_recv.at[g], mate),
            remote(tc.at[g], sx.at[g], tc_send.at[g], sx_recv.at[g], mate),
        )

    def d_copies(g):
        return (
            remote(od.at[g], rd.at[g], od_send.at[g], rd_recv.at[g], up),
            remote(td.at[g], sd.at[g], td_send.at[g], sd_recv.at[g], up),
        )

    def start(copies):
        for one in copies:
            one.start()

    lag, delay = 0, 4

    def step(i, carry):
        @pl.when(jnp.logical_and(i < groups, above))
        def _():
            remote(q.at[i], qd.at[i], qd_send.at[i], qd_recv.at[i], partner).wait_recv()

            @pl.when(even)
            def _():
                relay(i).start()

            def put(out, lse):
                od[i] = out.astype(jnp.bfloat16)
                ld[i] = lse

            @pl.when(k == 0)
            def _():
                put(*attend(qd[i], all_of(kall, i), all_of(vall, i), scale))

            @pl.when(k == 1)
            def _():
                put(*attend(qd[i], kall[i, 1], vall[i, 1], scale))

            @pl.when(odd)
            def _():
                td[i] = squeeze(ld[i], padded)
                start(d_copies(i))

        @pl.when(jnp.logical_and(jnp.logical_and(i >= lag, i < groups + lag), feeds))
        def _():
            g = i - lag
            remote(q.at[g], qc.at[g], qn_send.at[g], qc_recv.at[g], partner).wait_recv()
            o, lse = attend(qc[g], all_of(kall, g), all_of(vall, g), scale)
            oc[g] = o.astype(jnp.bfloat16)
            tc[g] = squeeze(lse, padded)

            @pl.when(even)
            def _():
                start(c_near(g))

            @pl.when(odd)
            def _():
                start(c_relay(g))

        @pl.when(i < groups)
        def _():
            @pl.when(k == 0)
            def _():
                own(i, kall[i, 0], vall[i, 0])

            @pl.when(k == 1)
            def _():
                own(i, all_of(kall, i), all_of(vall, i))

        @pl.when(jnp.logical_and(jnp.logical_and(i >= delay, even), above))
        def _():
            g = i - delay
            remote(oc.at[g], rx.at[g], oc_send.at[g], rx_recv.at[g], partner).wait_recv()
            remote(tc.at[g], sx.at[g], tc_send.at[g], sx_recv.at[g], partner).wait_recv()
            o, lse = merge([(od[g], ld[g]), (rx[g], widen(sx[g], capacity))])
            od[g] = o.astype(jnp.bfloat16)
            td[g] = squeeze(lse, padded)
            start(d_copies(g))

        return carry

    lax.fori_loop(0, groups + delay, step, 0)

    def absent(o, t):
        o[...] = jnp.zeros(o.shape, o.dtype)
        t[...] = jnp.full(t.shape, LOW, t.dtype)

    @pl.when(even)
    def _():
        absent(rc, sc)

    @pl.when(jnp.logical_not(below))
    def _():
        absent(rd, sd)

    def finish(g, carry):
        @pl.when(odd)
        def _():
            remote(oc.at[g], rc.at[g], oc_send.at[g], rc_recv.at[g], partner).wait_recv()
            remote(tc.at[g], sc.at[g], tc_send.at[g], sc_recv.at[g], partner).wait_recv()

        @pl.when(below)
        def _():
            remote(od.at[g], rd.at[g], od_send.at[g], rd_recv.at[g], partner).wait_recv()
            remote(td.at[g], sd.at[g], td_send.at[g], sd_recv.at[g], partner).wait_recv()

        parts = [
            (oa[g], la[g]), (rc[g], widen(sc[g], capacity)), (rd[g], widen(sd[g], capacity))
        ]
        fin[pl.ds(pl.multiple_of(g * capacity, 16), capacity), :] = merge(parts)[0].astype(jnp.bfloat16)
        return carry

    tile = 256
    tiles = groups * capacity // tile
    lane = lax.broadcasted_iota(jnp.int32, (tokens, tile), 1).astype(jnp.float32)
    done = 0
    stops = [2, 4, 6, 8] if groups == 8 else [groups]
    for s, stop in enumerate(stops):
        lax.fori_loop(stops[s - 1] if s else 0, stop, finish, 0)
        last = stop == groups
        upto = tiles if last else stop * capacity // tile
        for r in range(routed):
            slot = slots[:, r : r + 1]
            here = jnp.concatenate(
                [
                    (lane == slot - t * tile).astype(jnp.float32).astype(jnp.bfloat16)
                    for t in range(done, upto)
                ],
                axis=1,
            )
            part_sum = dot(here, fin[done * tile : upto * tile, :])
            total = part_sum if s == 0 else acc[r] + part_sum
            if last:
                wide[pl.ds(0, tokens), r, :] = total
            else:
                acc[r] = total
        done = upto
    out[...] = wide[pl.ds(0, tokens)].astype(jnp.bfloat16)

    for i in range(2):
        kv_copy(i).wait_send()

    def sent(there, make):
        @pl.when(there)
        def _():
            def body(g, carry):
                for one in make(g):
                    one.wait_send()
                return carry

            lax.fori_loop(0, groups, body, 0)

    sent(below, lambda g: (query_down(g),))
    sent(odd, lambda g: (query_near(g),))
    sent(jnp.logical_and(even, above), lambda g: (relay(g),))
    sent(above, d_copies)
    sent(even, c_near)
    sent(jnp.logical_and(odd, feeds), c_relay)


def shards(n, queries, keys, values, routes):
    tokens, routed, width = queries.shape
    context, groups, _ = keys.shape
    capacity = HEADS // groups * MOST
    padded = -(-capacity // LANES) * LANES
    vmem = pl.BlockSpec(memory_space=pltpu.VMEM)
    hbm = pl.BlockSpec(memory_space=pl.ANY)
    bf = lambda *shape: pltpu.VMEM(shape, jnp.bfloat16)
    f32 = lambda *shape: pltpu.VMEM(shape, jnp.float32)
    sem = lambda *shape: pltpu.SemaphoreType.DMA(shape)
    chunks = lambda: bf(groups, capacity, width)
    stats = lambda: f32(groups, 1, padded)
    full = lambda: f32(groups, capacity, width)
    return pl.pallas_call(
        functools.partial(kernel, n),
        out_shape=jax.ShapeDtypeStruct((tokens, routed, width), jnp.bfloat16),
        in_specs=[vmem, vmem, hbm, hbm],
        out_specs=vmem,
        scratch_shapes=[
            bf(2, context, groups, width), f32(tokens, groups, width), bf(routed * tokens, 2 * width),
            f32(routed, tokens), f32(tokens, LANES), chunks(), full(),
            bf(groups, 2, context, width), bf(groups, 2, context, width),
            chunks(), chunks(), full(), full(), chunks(), stats(), chunks(), full(), stats(),
            chunks(), stats(), chunks(), stats(), chunks(), stats(),
            bf(groups * capacity, width), f32(routed, tokens, width),
        ] + [sem(2)] * 3 + [sem(groups)] * 15,
        compiler_params=pltpu.CompilerParams(
            collective_id=0, has_side_effects=True, vmem_limit_bytes=60 * 1024 * 1024
        ),
        name="fused",
    )(queries, routes.T, keys, values)


def solution(mesh):
    n = mesh.shape["seq"]
    placed = (P("seq", None, None), P("seq", None, None), P("seq", None, None), P("seq", None))
    return jax.shard_map(
        functools.partial(shards, n),
        mesh=mesh,
        in_specs=placed,
        out_specs=P("seq", None, None),
        check_vma=False,
    )
```

time: 68 us -> 59.9 us (0.88)
  the two profiles are of different devices: /device:TPU:21 before, /device:TPU:0 now
where the time goes in v1:
time: 59.9 us; the launch traced here: 59.7 us
  Pallas kernels  57.9 us (97%)
  local copies, waits for them, and re-layouts  1.87 us (3%)
    pallas_call x1, Pallas kernels, shards(): pl.pallas_call(functools.partial(kernel, n), out_shape=jax.ShapeDtypeStru...  57.9 us
    unnamed x1, local copies, waits for them, and re-layouts  1.87 us

profile of v1, /device:TPU:0, one launch (start us, length us, event | category | flops | bytes accessed | tf_op | source)
XLA Modules:
  0.0 59.7 jit_solution(992210624625101869)
XLA Ops:
  0.0 57.9 %fused.1 = bf16[256,8,128]{2,1,0:T(8,128)(2,1)} custom-call(bf16[256,8,128]{2,1,0:T(8,128)(2,1)} %q_in.1, s32[8,256]{1,0:T(8,128)} %bitcast.1, bf16[512,8,128]{2,1,0:T(8,128)(2,1)} %k_hbm.1, bf16[512,8,128]{2,1,0:T(8,128)(2,1)} %v_hbm.1), custom_call_target="tpu_custom_call" | custom-call | tf_op jit(solution)/shard_map/fused/pallas_call | solution.py:393
  57.9 1.9 %copy.6 = bf16[256,8,128]{2,1,0:T(8,128)(2,1)} copy(bf16[256,8,128]{2,1,0:T(8,128)(2,1)} %fused.1) | data formatting | bytes 1048576

commit v2 on v1

--- a/solution.py
+++ b/solution.py
@@ -62,14 +62,15 @@
 
 def kernel(
     n, q_in, routes_t, k_hbm, v_hbm, out,
-    raw, wide, rights, slot_rows, slots, q, pos, kall, vall,
-    qc, qd, oa, la, oc, tc, od, ld, td, rx, sx, rc, sc, rd, sd, fin, acc,
+    raw, wide, rights, slot_rows, slots, qq, pos, kall, vall,
+    qc, op, lp, oc, tc, od, td, rx, sx, rc, sc, rd, sd, fin, acc,
     raw_sem, kv_send, kv_recv, qn_send, qd_send, qc_recv, qd_recv, relay_send,
     oc_send, tc_send, od_send, td_send,
     rx_recv, sx_recv, rc_recv, sc_recv, rd_recv, sd_recv,
 ):
     tokens, routed, width = q_in.shape
-    groups, capacity, _ = q.shape
+    groups, capacity = qq.shape[1:3]
+    q, qd = qq.at[1], qq.at[0]
     context = kall.shape[2]
     padded = tc.shape[2]
     per_group = HEADS // groups
@@ -124,10 +125,10 @@
     slot_rows[...] = slot_all
     slots[...] = jnp.concatenate([slot_all] * (LANES // routed), axis=0).T
 
-    wide[pl.ds(0, tokens)] = q_in[...].astype(jnp.float32)
+    wide[pl.ds(0, tokens * routed), :] = q_in[...].astype(jnp.float32).reshape(tokens * routed, width)
     token = lax.broadcasted_iota(jnp.int32, (tokens, width), 0).astype(jnp.float32).astype(jnp.bfloat16)
     for r in range(routed):
-        rights[pl.ds(r * tokens, tokens), :width] = wide[pl.ds(0, tokens), r, :].astype(jnp.bfloat16)
+        rights[pl.ds(r * tokens, tokens), :width] = wide[pl.ds(r, tokens, stride=routed), :].astype(jnp.bfloat16)
         rights[pl.ds(r * tokens, tokens), width:] = token
 
     pl.semaphore_wait(barrier, 2 + below.astype(jnp.int32) + above.astype(jnp.int32))
@@ -170,9 +171,9 @@
     def turn(i, to):
         def body(s, carry):
             at = pl.multiple_of(s * part, part)
-            wide[pl.ds(0, part)] = raw[i, pl.ds(at, part)].astype(jnp.float32)
+            wide[pl.ds(0, part * groups), :] = raw[i, pl.ds(at, part)].astype(jnp.float32).reshape(part * groups, width)
             for g in range(groups):
-                to[g, k, pl.ds(at, part), :] = wide[pl.ds(0, part), g, :].astype(jnp.bfloat16)
+                to[g, k, pl.ds(at, part), :] = wide[pl.ds(g, part, stride=groups), :].astype(jnp.bfloat16)
             return carry
 
         lax.fori_loop(0, context // part, body, 0)
@@ -197,15 +198,30 @@
     def all_of(a, g):
         return a[g].reshape(2 * context, width)
 
-    def own(g, keys, values):
-        limit = jnp.concatenate([pos[g]] * (tokens // LANES), axis=1)
-
-        def mask(s):
-            free = s.shape[1] - tokens
-            tail = jnp.where(column <= limit, s[:, free:], jnp.float32(LOW))
-            return jnp.concatenate([s[:, :free], tail], axis=1)
-
-        oa[g], la[g] = attend(q[g], keys, values, scale, mask)
+    def masked(bias):
+        def of(g):
+            limit = jnp.concatenate([pos[g] + bias] * (tokens // LANES), axis=1)
+
+            def mask(x):
+                free = x.shape[1] - tokens
+                tail = jnp.where(column <= limit, x[:, free:], jnp.float32(LOW))
+                return jnp.concatenate([x[:, :free], tail], axis=1)
+
+            return mask
+
+        return of
+
+    first = masked(jnp.where(k == 1, jnp.float32(0), jnp.float32(2 * tokens)))
+    second = masked(jnp.where(k == 0, jnp.float32(0), jnp.float32(2 * tokens)))
+
+    def both_shards(g):
+        return attend(qq[k, g], all_of(kall, g), all_of(vall, g), scale, first(g))
+
+    def one_shard(g):
+        return attend(qq[1 - k, g], kall[g, k], vall[g, k], scale, second(g))
+
+    def nearer(g):
+        return attend(qc[g], all_of(kall, g), all_of(vall, g), scale)
 
     def relay(g):
         return remote(qd.at[g], qc.at[g], relay_send.at[g], qc_recv.at[g], mate)
@@ -232,73 +248,106 @@
         for one in copies:
             one.start()
 
-    lag, delay = 0, 4
-
-    def step(i, carry):
-        @pl.when(jnp.logical_and(i < groups, above))
-        def _():
-            remote(q.at[i], qd.at[i], qd_send.at[i], qd_recv.at[i], partner).wait_recv()
-
-            @pl.when(even)
-            def _():
-                relay(i).start()
-
-            def put(out, lse):
-                od[i] = out.astype(jnp.bfloat16)
-                ld[i] = lse
-
-            @pl.when(k == 0)
-            def _():
-                put(*attend(qd[i], all_of(kall, i), all_of(vall, i), scale))
-
-            @pl.when(k == 1)
-            def _():
-                put(*attend(qd[i], kall[i, 1], vall[i, 1], scale))
-
-            @pl.when(odd)
-            def _():
-                td[i] = squeeze(ld[i], padded)
-                start(d_copies(i))
-
-        @pl.when(jnp.logical_and(jnp.logical_and(i >= lag, i < groups + lag), feeds))
-        def _():
-            g = i - lag
-            remote(q.at[g], qc.at[g], qn_send.at[g], qc_recv.at[g], partner).wait_recv()
-            o, lse = attend(qc[g], all_of(kall, g), all_of(vall, g), scale)
+    @pl.when(jnp.logical_not(above))
+    def _():
+        qq[0] = jnp.zeros(qq.shape[1:], qq.dtype)
+
+    @pl.when(jnp.logical_not(feeds))
+    def _():
+        qc[...] = jnp.zeros(qc.shape, qc.dtype)
+
+    pair = 2
+    steps = groups // pair
+
+    def arrive_far(i):
+        @pl.when(above)
+        def _():
+            for u in range(pair):
+                g = i * pair + u
+                remote(q.at[g], qd.at[g], qd_send.at[g], qd_recv.at[g], partner).wait_recv()
+
+                @pl.when(even)
+                def _():
+                    relay(g).start()
+
+    def arrive_near(i):
+        @pl.when(feeds)
+        def _():
+            for u in range(pair):
+                g = i * pair + u
+                remote(q.at[g], qc.at[g], qn_send.at[g], qc_recv.at[g], partner).wait_recv()
+
+    def send_far(i):
+        @pl.when(jnp.logical_and(odd, above))
+        def _():
+            for u in range(pair):
+                g = i * pair + u
+                od[g] = op[0, g].astype(jnp.bfloat16)
+                td[g] = squeeze(lp[0, g], padded)
+                start(d_copies(g))
+
+    def send_near(i):
+        @pl.when(even)
+        def _():
+            for u in range(pair):
+                start(c_near(i * pair + u))
+
+    def send_relay(i):
+        @pl.when(jnp.logical_and(odd, feeds))
+        def _():
+            for u in range(pair):
+                start(c_relay(i * pair + u))
+
+    def block(far, near):
+        got = []
+        if far is not None:
+            for u in range(pair):
+                g = far * pair + u
+                got.append((k, g, both_shards(g)))
+                got.append((1 - k, g, one_shard(g)))
+        close = []
+        if near is not None:
+            for u in range(pair):
+                close.append((near * pair + u, nearer(near * pair + u)))
+        for at, g, (o, lse) in got:
+            op[at, g] = o
+            lp[at, g] = lse
+        for g, (o, lse) in close:
             oc[g] = o.astype(jnp.bfloat16)
             tc[g] = squeeze(lse, padded)
 
-            @pl.when(even)
-            def _():
-                start(c_near(g))
-
-            @pl.when(odd)
-            def _():
-                start(c_relay(g))
-
-        @pl.when(i < groups)
-        def _():
-            @pl.when(k == 0)
-            def _():
-                own(i, kall[i, 0], vall[i, 0])
-
-            @pl.when(k == 1)
-            def _():
-                own(i, all_of(kall, i), all_of(vall, i))
-
-        @pl.when(jnp.logical_and(jnp.logical_and(i >= delay, even), above))
-        def _():
-            g = i - delay
+    arrive_far(0)
+    block(0, None)
+    send_far(0)
+
+    def step(i, carry):
+        arrive_far(i)
+        arrive_near(i - 1)
+        block(i, i - 1)
+        send_far(i)
+        send_relay(i - 1)
+        return carry
+
+    lax.fori_loop(1, steps, step, 0)
+    for i in range(steps - 1):
+        send_near(i)
+    arrive_near(steps - 1)
+    block(None, steps - 1)
+    send_near(steps - 1)
+    send_relay(steps - 1)
+
+    @pl.when(jnp.logical_and(even, above))
+    def _():
+        def join(g, carry):
             remote(oc.at[g], rx.at[g], oc_send.at[g], rx_recv.at[g], partner).wait_recv()
             remote(tc.at[g], sx.at[g], tc_send.at[g], sx_recv.at[g], partner).wait_recv()
-            o, lse = merge([(od[g], ld[g]), (rx[g], widen(sx[g], capacity))])
+            o, lse = merge([(op[0, g], lp[0, g]), (rx[g], widen(sx[g], capacity))])
             od[g] = o.astype(jnp.bfloat16)
             td[g] = squeeze(lse, padded)
             start(d_copies(g))
-
-        return carry
-
-    lax.fori_loop(0, groups + delay, step, 0)
+            return carry
+
+        lax.fori_loop(0, groups, join, 0)
 
     def absent(o, t):
         o[...] = jnp.zeros(o.shape, o.dtype)
@@ -324,7 +373,7 @@
             remote(td.at[g], sd.at[g], td_send.at[g], sd_recv.at[g], partner).wait_recv()
 
         parts = [
-            (oa[g], la[g]), (rc[g], widen(sc[g], capacity)), (rd[g], widen(sd[g], capacity))
+            (op[1, g], lp[1, g]), (rc[g], widen(sc[g], capacity)), (rd[g], widen(sd[g], capacity))
         ]
         fin[pl.ds(pl.multiple_of(g * capacity, 16), capacity), :] = merge(parts)[0].astype(jnp.bfloat16)
         return carry
@@ -339,10 +388,10 @@
         last = stop == groups
         upto = tiles if last else stop * capacity // tile
         for r in range(routed):
-            slot = slots[:, r : r + 1]
+            slot = jnp.broadcast_to(slots[:, r : r + 1], (tokens, tile))
             here = jnp.concatenate(
                 [
-                    (lane == slot - t * tile).astype(jnp.float32).astype(jnp.bfloat16)
+                    (lane + t * tile == slot).astype(jnp.float32).astype(jnp.bfloat16)
                     for t in range(done, upto)
                 ],
                 axis=1,
@@ -350,11 +399,11 @@
             part_sum = dot(here, fin[done * tile : upto * tile, :])
             total = part_sum if s == 0 else acc[r] + part_sum
             if last:
-                wide[pl.ds(0, tokens), r, :] = total
+                wide[pl.ds(r, tokens, stride=routed), :] = total
             else:
                 acc[r] = total
         done = upto
-    out[...] = wide[pl.ds(0, tokens)].astype(jnp.bfloat16)
+    out[...] = wide[pl.ds(0, tokens * routed), :].reshape(tokens, routed, width).astype(jnp.bfloat16)
 
     for i in range(2):
         kv_copy(i).wait_send()
@@ -396,10 +445,11 @@
         in_specs=[vmem, vmem, hbm, hbm],
         out_specs=vmem,
         scratch_shapes=[
-            bf(2, context, groups, width), f32(tokens, groups, width), bf(routed * tokens, 2 * width),
-            f32(routed, tokens), f32(tokens, LANES), chunks(), full(),
+            bf(2, context, groups, width), f32(max(tokens * routed, LANES * groups), width), bf(routed * tokens, 2 * width),
+            f32(routed, tokens), f32(tokens, LANES), bf(2, groups, capacity, width), full(),
             bf(groups, 2, context, width), bf(groups, 2, context, width),
-            chunks(), chunks(), full(), full(), chunks(), stats(), chunks(), full(), stats(),
+            chunks(), f32(2, groups, capacity, width), f32(2, groups, capacity, width),
+            chunks(), stats(), chunks(), stats(),
             chunks(), stats(), chunks(), stats(), chunks(), stats(),
             bf(groups * capacity, width), f32(routed, tokens, width),
         ] + [sem(2)] * 3 + [sem(groups)] * 15,

time: 59.9 us -> 53 us (0.88)
  the two profiles are of different devices: /device:TPU:0 before, /device:TPU:8 now
where the time goes in v2:
time: 53 us; the launch traced here: 52.8 us
  Pallas kernels  50.9 us (96%)
  local copies, waits for them, and re-layouts  1.87 us (4%)
    pallas_call x1, Pallas kernels, shards(): pl.pallas_call(functools.partial(kernel, n), out_shape=jax.ShapeDtypeStru...  50.9 us
    unnamed x1, local copies, waits for them, and re-layouts  1.87 us

profile of v2, /device:TPU:8, one launch (start us, length us, event | category | flops | bytes accessed | tf_op | source)
XLA Modules:
  0.0 52.8 jit_solution(12517060909912890793)
XLA Ops:
  0.0 50.9 %fused.1 = bf16[256,8,128]{2,1,0:T(8,128)(2,1)} custom-call(bf16[256,8,128]{2,1,0:T(8,128)(2,1)} %q_in.1, s32[8,256]{1,0:T(8,128)} %bitcast.1, bf16[512,8,128]{2,1,0:T(8,128)(2,1)} %k_hbm.1, bf16[512,8,128]{2,1,0:T(8,128)(2,1)} %v_hbm.1), custom_call_target="tpu_custom_call" | custom-call | tf_op jit(solution)/shard_map/fused/pallas_call | solution.py:442
  50.9 1.9 %copy.6 = bf16[256,8,128]{2,1,0:T(8,128)(2,1)} copy(bf16[256,8,128]{2,1,0:T(8,128)(2,1)} %fused.1) | data formatting | bytes 1048576

commit v3 on v2

--- a/solution.py
+++ b/solution.py
@@ -284,13 +284,22 @@
                 g = i * pair + u
                 od[g] = op[0, g].astype(jnp.bfloat16)
                 td[g] = squeeze(lp[0, g], padded)
-                start(d_copies(g))
-
-    def send_near(i):
+
+    def release(upto_far, upto_near, from_far=0, from_near=0):
+        def go(make, a, b):
+            def body(g, carry):
+                start(make(g))
+                return carry
+
+            lax.fori_loop(a * pair, b * pair, body, 0)
+
+        @pl.when(jnp.logical_and(odd, above))
+        def _():
+            go(d_copies, from_far, upto_far)
+
         @pl.when(even)
         def _():
-            for u in range(pair):
-                start(c_near(i * pair + u))
+            go(c_near, from_near, upto_near)
 
     def send_relay(i):
         @pl.when(jnp.logical_and(odd, feeds))
@@ -322,6 +331,11 @@
 
     def step(i, carry):
         arrive_far(i)
+
+        @pl.when(i == steps - 1)
+        def _():
+            release(steps - 1, steps - 2)
+
         arrive_near(i - 1)
         block(i, i - 1)
         send_far(i)
@@ -329,11 +343,10 @@
         return carry
 
     lax.fori_loop(1, steps, step, 0)
-    for i in range(steps - 1):
-        send_near(i)
+    release(steps, steps - 1, steps - 1, steps - 2)
     arrive_near(steps - 1)
     block(None, steps - 1)
-    send_near(steps - 1)
+    release(steps, steps, steps, steps - 1)
     send_relay(steps - 1)
 
     @pl.when(jnp.logical_and(even, above))

time: 53 us -> 47.4 us (0.89)
  the two profiles are of different devices: /device:TPU:8 before, /device:TPU:0 now
where the time goes in v3:
time: 47.4 us; the launch traced here: 47.2 us
  Pallas kernels  45.3 us (96%)
  local copies, waits for them, and re-layouts  1.87 us (4%)
    pallas_call x1, Pallas kernels, shards(): pl.pallas_call(functools.partial(kernel, n), out_shape=jax.ShapeDtypeStru...  45.3 us
    unnamed x1, local copies, waits for them, and re-layouts  1.87 us

profile of v3, /device:TPU:0, one launch (start us, length us, event | category | flops | bytes accessed | tf_op | source)
XLA Modules:
  0.0 47.2 jit_solution(13111154229453044034)
XLA Ops:
  0.0 45.3 %fused.1 = bf16[256,8,128]{2,1,0:T(8,128)(2,1)} custom-call(bf16[256,8,128]{2,1,0:T(8,128)(2,1)} %q_in.1, s32[8,256]{1,0:T(8,128)} %bitcast.1, bf16[512,8,128]{2,1,0:T(8,128)(2,1)} %k_hbm.1, bf16[512,8,128]{2,1,0:T(8,128)(2,1)} %v_hbm.1), custom_call_target="tpu_custom_call" | custom-call | tf_op jit(solution)/shard_map/fused/pallas_call | solution.py:455
  45.3 1.9 %copy.6 = bf16[256,8,128]{2,1,0:T(8,128)(2,1)} copy(bf16[256,8,128]{2,1,0:T(8,128)(2,1)} %fused.1) | data formatting | bytes 1048576

commit v4 on v3

--- a/solution.py
+++ b/solution.py
@@ -61,10 +61,10 @@
 
 
 def kernel(
-    n, q_in, routes_t, k_hbm, v_hbm, out,
-    raw, wide, rights, slot_rows, slots, qq, pos, kall, vall,
+    n, q_hbm, routes_hbm, k_hbm, v_hbm, out,
+    q_in, routes_t, raw, wide, rights, slot_rows, slots, qq, pos, kall, vall,
     qc, op, lp, oc, tc, od, td, rx, sx, rc, sc, rd, sd, fin, acc,
-    raw_sem, kv_send, kv_recv, qn_send, qd_send, qc_recv, qd_recv, relay_send,
+    in_sem, raw_sem, kv_send, kv_recv, qn_send, qd_send, qc_recv, qd_recv, relay_send,
     oc_send, tc_send, od_send, td_send,
     rx_recv, sx_recv, rc_recv, sc_recv, rd_recv, sd_recv,
 ):
@@ -105,9 +105,14 @@
     def _():
         signal(up)
 
+    ins = [
+        pltpu.make_async_copy(a, b, in_sem.at[i])
+        for i, (a, b) in enumerate(((routes_hbm, routes_t), (q_hbm, q_in)))
+    ]
     raws = [pltpu.make_async_copy(a, raw.at[i], raw_sem.at[i]) for i, a in enumerate((k_hbm, v_hbm))]
-    for one in raws:
+    for one in ins + raws:
         one.start()
+    ins[0].wait()
 
     group_of = routes_t[...] // per_group
     group = lax.broadcasted_iota(jnp.int32, (groups, tokens), 0)
@@ -125,6 +130,7 @@
     slot_rows[...] = slot_all
     slots[...] = jnp.concatenate([slot_all] * (LANES // routed), axis=0).T
 
+    ins[1].wait()
     wide[pl.ds(0, tokens * routed), :] = q_in[...].astype(jnp.float32).reshape(tokens * routed, width)
     token = lax.broadcasted_iota(jnp.int32, (tokens, width), 0).astype(jnp.float32).astype(jnp.bfloat16)
     for r in range(routed):
@@ -349,6 +355,23 @@
     release(steps, steps, steps, steps - 1)
     send_relay(steps - 1)
 
+    for i in range(2):
+        kv_copy(i).wait_send()
+
+    def sent(there, make):
+        @pl.when(there)
+        def _():
+            def body(g, carry):
+                for one in make(g):
+                    one.wait_send()
+                return carry
+
+            lax.fori_loop(0, groups, body, 0)
+
+    sent(below, lambda g: (query_down(g),))
+    sent(odd, lambda g: (query_near(g),))
+    sent(jnp.logical_and(even, above), lambda g: (relay(g),))
+
     @pl.when(jnp.logical_and(even, above))
     def _():
         def join(g, carry):
@@ -391,11 +414,13 @@
         fin[pl.ds(pl.multiple_of(g * capacity, 16), capacity), :] = merge(parts)[0].astype(jnp.bfloat16)
         return carry
 
+    sent(jnp.logical_and(odd, feeds), c_relay)
+
     tile = 256
     tiles = groups * capacity // tile
     lane = lax.broadcasted_iota(jnp.int32, (tokens, tile), 1).astype(jnp.float32)
     done = 0
-    stops = [2, 4, 6, 8] if groups == 8 else [groups]
+    stops = [2, 4, 6, 7, 8] if groups == 8 else [groups]
     for s, stop in enumerate(stops):
         lax.fori_loop(stops[s - 1] if s else 0, stop, finish, 0)
         last = stop == groups
@@ -418,25 +443,8 @@
         done = upto
     out[...] = wide[pl.ds(0, tokens * routed), :].reshape(tokens, routed, width).astype(jnp.bfloat16)
 
-    for i in range(2):
-        kv_copy(i).wait_send()
-
-    def sent(there, make):
-        @pl.when(there)
-        def _():
-            def body(g, carry):
-                for one in make(g):
-                    one.wait_send()
-                return carry
-
-            lax.fori_loop(0, groups, body, 0)
-
-    sent(below, lambda g: (query_down(g),))
-    sent(odd, lambda g: (query_near(g),))
-    sent(jnp.logical_and(even, above), lambda g: (relay(g),))
     sent(above, d_copies)
     sent(even, c_near)
-    sent(jnp.logical_and(odd, feeds), c_relay)
 
 
 def shards(n, queries, keys, values, routes):
@@ -445,7 +453,7 @@
     capacity = HEADS // groups * MOST
     padded = -(-capacity // LANES) * LANES
     vmem = pl.BlockSpec(memory_space=pltpu.VMEM)
-    hbm = pl.BlockSpec(memory_space=pl.ANY)
+    hbm = pl.BlockSpec(memory_space=pltpu.HBM)
     bf = lambda *shape: pltpu.VMEM(shape, jnp.bfloat16)
     f32 = lambda *shape: pltpu.VMEM(shape, jnp.float32)
     sem = lambda *shape: pltpu.SemaphoreType.DMA(shape)
@@ -455,9 +463,10 @@
     return pl.pallas_call(
         functools.partial(kernel, n),
         out_shape=jax.ShapeDtypeStruct((tokens, routed, width), jnp.bfloat16),
-        in_specs=[vmem, vmem, hbm, hbm],
+        in_specs=[hbm] * 4,
         out_specs=vmem,
         scratch_shapes=[
+            bf(tokens, routed, width), pltpu.VMEM((routed, tokens), jnp.int32),
             bf(2, context, groups, width), f32(max(tokens * routed, LANES * groups), width), bf(routed * tokens, 2 * width),
             f32(routed, tokens), f32(tokens, LANES), bf(2, groups, capacity, width), full(),
             bf(groups, 2, context, width), bf(groups, 2, context, width),
@@ -465,12 +474,12 @@
             chunks(), stats(), chunks(), stats(),
             chunks(), stats(), chunks(), stats(), chunks(), stats(),
             bf(groups * capacity, width), f32(routed, tokens, width),
-        ] + [sem(2)] * 3 + [sem(groups)] * 15,
+        ] + [sem(2)] * 4 + [sem(groups)] * 15,
         compiler_params=pltpu.CompilerParams(
-            collective_id=0, has_side_effects=True, vmem_limit_bytes=60 * 1024 * 1024
+            collective_id=0, has_side_effects=True, vmem_limit_bytes=48 * 1024 * 1024
         ),
         name="fused",
-    )(queries, routes.T, keys, values)
+    )(*(pltpu.with_memory_space_constraint(a, pltpu.HBM) for a in (queries, routes.T, keys, values)))
 
 
 def solution(mesh):

time: 47.4 us -> 45 us (0.949)
  the two profiles are of different devices: /device:TPU:0 before, /device:TPU:8 now
where the time goes in v4:
time: 45 us; the launch traced here: 44.8 us
  Pallas kernels  44 us (98%)
  local copies, waits for them, and re-layouts  0.8 us (2%)
    pallas_call x1, Pallas kernels, shards(): pl.pallas_call(functools.partial(kernel, n), out_shape=jax.ShapeDtypeStru...  44 us

profile of v4, /device:TPU:8, one launch (start us, length us, event | category | flops | bytes accessed | tf_op | source)
XLA Modules:
  0.0 44.8 jit_solution(970496497505521084)
XLA Ops:
  0.0 44.0 %fused.1 = bf16[256,8,128]{2,1,0:T(8,128)(2,1)S(1)} custom-call(bf16[256,8,128]{2,1,0:T(8,128)(2,1)} %q_hbm.1, s32[8,256]{1,0:T(8,128)} %bitcast.1, bf16[512,8,128]{2,1,0:T(8,128)(2,1)} %k_hbm.1, bf16[512,8,128]{2,1,0:T(8,128)(2,1)} %v_hbm.1), custom_call_target="tpu_custom_call" | custom-call | tf_op jit(solution)/shard_map/fused/pallas_call | solution.py:463
  44.0 0.8 %copy.6 = bf16[256,8,128]{2,1,0:T(8,128)(2,1)} copy(bf16[256,8,128]{2,1,0:T(8,128)(2,1)S(1)} %fused.1) | data formatting | bytes 1048576

commit v5 on v4

--- a/solution.py
+++ b/solution.py
@@ -12,6 +12,8 @@
 MOST = 40
 LANES = 128
 LOW = -1e30
+BLOCK = 16
+TABLE = 256
 MESH = pl.DeviceIdType.MESH
 
 
@@ -62,15 +64,17 @@
 
 def kernel(
     n, q_hbm, routes_hbm, k_hbm, v_hbm, out,
-    q_in, routes_t, raw, wide, rights, slot_rows, slots, qq, pos, kall, vall,
-    qc, op, lp, oc, tc, od, td, rx, sx, rc, sc, rd, sd, fin, acc,
-    in_sem, raw_sem, kv_send, kv_recv, qn_send, qd_send, qc_recv, qd_recv, relay_send,
+    q_in, routes_t, raw, wide, rights, slot_rows, slots, wq, wc, pos, kall, vall,
+    tab, tab_d, tab_c, at_own, at_d, at_c,
+    qd, qc, op, lp, cp, lc, oc, tc, od, td, rx, sx, rc, sc, rd, sd, fin, acc,
+    in_sem, tab_sem, tab_far, tab_near, tab_relay, raw_sem, kv_send, kv_recv, qn_send, qd_send, qc_recv, qd_recv, relay_send,
     oc_send, tc_send, od_send, td_send,
     rx_recv, sx_recv, rc_recv, sc_recv, rd_recv, sd_recv,
 ):
     tokens, routed, width = q_in.shape
-    groups, capacity = qq.shape[1:3]
-    q, qd = qq.at[1], qq.at[0]
+    groups = kall.shape[0]
+    chunks, per_block = qd.shape[:2]
+    capacity = per_block * BLOCK
     context = kall.shape[2]
     padded = tc.shape[2]
     per_group = HEADS // groups
@@ -121,7 +125,25 @@
     row = lax.broadcasted_iota(jnp.int32, (tokens, tokens), 0)
     col = lax.broadcasted_iota(jnp.int32, (tokens, tokens), 1)
     upper = (row < col).astype(jnp.float32).astype(jnp.bfloat16)
-    rank = dot(count.astype(jnp.bfloat16), upper) + (group * capacity).astype(jnp.float32)
+    many = functools.reduce(
+        jnp.add, [(group_of[r : r + 1] == group).astype(jnp.int32) for r in range(routed)]
+    )
+    blocks = (jnp.sum(many, axis=1, keepdims=True) + (BLOCK - 1)) // BLOCK
+    blocks = jnp.broadcast_to(blocks, (groups, TABLE))
+    starts = [jnp.zeros((1, TABLE), jnp.int32)]
+    for g in range(1, groups):
+        starts.append(starts[-1] + blocks[g - 1 : g])
+    place = lax.broadcasted_iota(jnp.int32, (1, TABLE), 1)
+    source = place
+    first_block = starts[0]
+    for g in range(1, groups):
+        source = source + jnp.where(place >= starts[g], per_block - blocks[g - 1 : g], 0)
+        first_block = jnp.where(place >= g, starts[g], first_block)
+    source = jnp.minimum(source, groups * per_block - 1)
+    first_block = jnp.minimum(first_block, chunks * per_block)
+    tab[...] = jnp.concatenate([source, first_block], axis=1)
+    base = jnp.concatenate(starts, axis=0)[:, :1].astype(jnp.float32) * BLOCK
+    rank = dot(count.astype(jnp.bfloat16), upper) + base
     rows = []
     for r in range(routed):
         rows.append(jnp.sum(hots[r] * rank, axis=0, keepdims=True))
@@ -139,11 +161,62 @@
 
     pl.semaphore_wait(barrier, 2 + below.astype(jnp.int32) + above.astype(jnp.int32))
 
-    def query_down(g):
-        return remote(q.at[g], qd.at[g], qd_send.at[g], qd_recv.at[g], down)
-
-    def query_near(g):
-        return remote(q.at[g], qc.at[g], qn_send.at[g], qc_recv.at[g], mate)
+    def rows_of(j):
+        return pl.ds(j * per_block, per_block)
+
+    def split(x):
+        return x.reshape(x.shape[0] // BLOCK, BLOCK, width)
+
+    def flat(x):
+        return x.reshape(x.shape[0] * BLOCK, width)
+
+    halves = 2
+    part_rows = per_block // halves
+
+    def part_of(h):
+        return pl.ds(h * part_rows, part_rows)
+
+    def query_part(j, h):
+        return wq.at[1, pl.ds(j * per_block + h * part_rows, part_rows)]
+
+    def query_down(j):
+        return [
+            remote(query_part(j, h), qd.at[j, part_of(h)], qd_send.at[j, h], qd_recv.at[j, h], down)
+            for h in range(halves)
+        ]
+
+    def query_near(j):
+        return [
+            remote(query_part(j, h), qc.at[j, part_of(h)], qn_send.at[j, h], qc_recv.at[j, h], mate)
+            for h in range(halves)
+        ]
+
+    def relay_part(j, h):
+        return remote(qd.at[j, part_of(h)], qc.at[j, part_of(h)], relay_send.at[j, h], qc_recv.at[j, h], mate)
+
+    def relay(j):
+        return [relay_part(j, h) for h in range(halves)]
+
+    def start(copies):
+        for one in copies:
+            one.start()
+
+    def table_down():
+        return remote(tab, tab_d, tab_far.at[0], tab_far.at[1], down)
+
+    def table_near():
+        return remote(tab, tab_c, tab_near.at[0], tab_near.at[1], mate)
+
+    def table_relay():
+        return remote(tab_d, tab_c, tab_relay.at[0], tab_near.at[1], mate)
+
+    @pl.when(below)
+    def _():
+        table_down().start()
+
+    @pl.when(odd)
+    def _():
+        table_near().start()
 
     place = lax.broadcasted_iota(jnp.int32, (capacity, tokens), 0).astype(jnp.float32)
 
@@ -157,20 +230,82 @@
             axis=1,
         )
         both = dot(here, rights[...])
-        q[g] = both[:, :width].astype(jnp.bfloat16)
-        pos[g] = both[:, width:]
+        wq[1, rows_of(g)] = split(both[:, :width].astype(jnp.bfloat16))
+        pos[rows_of(g)] = split(both[:, width:])
 
         @pl.when(below)
         def _():
-            query_down(g).start()
+            start(query_down(g))
 
         @pl.when(odd)
         def _():
-            query_near(g).start()
+            start(query_near(g))
 
         return carry
 
-    lax.fori_loop(0, groups, pack, 0)
+    lax.fori_loop(0, chunks, pack, 0)
+
+    local = [
+        pltpu.make_async_copy(a, b, tab_sem.at[i])
+        for i, (a, b) in enumerate(((tab_d, at_d), (tab, at_own), (tab_c, at_c)))
+    ]
+    local[1].start()
+    rest = (groups - chunks) * per_block
+    wq[1, pl.ds(chunks * per_block, rest)] = jnp.zeros((rest, BLOCK, width), wq.dtype)
+    pos[pl.ds(chunks * per_block, rest)] = jnp.zeros((rest, BLOCK, width), pos.dtype)
+    wq[0] = jnp.zeros(wq.shape[1:], wq.dtype)
+    wc[...] = jnp.zeros(wc.shape, wc.dtype)
+
+    def each(a, b, body):
+        def go(j, carry):
+            body(j)
+            return carry
+
+        lax.fori_loop(a, b, go, 0)
+
+    @pl.when(above)
+    def _():
+        remote(tab, tab_d, tab_far.at[0], tab_far.at[1], partner).wait_recv()
+
+        @pl.when(even)
+        def _():
+            table_relay().start()
+
+    @pl.when(jnp.logical_not(above))
+    def _():
+        tab_d[...] = tab[...]
+
+    local[0].start()
+    local[0].wait()
+    local[1].wait()
+
+    def absent(o, t):
+        o[...] = jnp.zeros(o.shape, o.dtype)
+        t[...] = jnp.full(t.shape, LOW, t.dtype)
+
+    @pl.when(even)
+    def _():
+        absent(rc, sc)
+
+    @pl.when(jnp.logical_not(below))
+    def _():
+        absent(rd, sd)
+
+    def far_chunk(j):
+        @pl.when(jnp.logical_and(above, j < chunks))
+        def _():
+            for h in range(halves):
+                remote(
+                    qd.at[j, part_of(h)], qd.at[j, part_of(h)], qd_send.at[j, h], qd_recv.at[j, h], partner
+                ).wait_recv()
+
+                @pl.when(even)
+                def _(h=h):
+                    relay_part(j, h).start()
+
+            wq[0, rows_of(j)] = qd[j]
+
+    far_chunk(jnp.int32(0))
 
     part = 128
 
@@ -196,6 +331,7 @@
         raws[i].wait()
         turn(i, to)
         kv_copy(i).start()
+    far_chunk(jnp.int32(1))
     for i in range(2):
         kv_arrival(i).wait_recv()
 
@@ -204,9 +340,13 @@
     def all_of(a, g):
         return a[g].reshape(2 * context, width)
 
+    def window(table, g):
+        return pl.ds(table[0, TABLE + g], per_block)
+
     def masked(bias):
         def of(g):
-            limit = jnp.concatenate([pos[g] + bias] * (tokens // LANES), axis=1)
+            limit = flat(pos[window(at_own, g)]) + bias
+            limit = jnp.concatenate([limit] * (tokens // LANES), axis=1)
 
             def mask(x):
                 free = x.shape[1] - tokens
@@ -220,17 +360,21 @@
     first = masked(jnp.where(k == 1, jnp.float32(0), jnp.float32(2 * tokens)))
     second = masked(jnp.where(k == 0, jnp.float32(0), jnp.float32(2 * tokens)))
 
+    def queries_of(which, g):
+        at = jnp.where(which == 1, at_own[0, TABLE + g], at_d[0, TABLE + g])
+        return flat(wq[which, pl.ds(at, per_block)])
+
     def both_shards(g):
-        return attend(qq[k, g], all_of(kall, g), all_of(vall, g), scale, first(g))
+        return attend(queries_of(k, g), all_of(kall, g), all_of(vall, g), scale, first(g))
 
     def one_shard(g):
-        return attend(qq[1 - k, g], kall[g, k], vall[g, k], scale, second(g))
+        return attend(queries_of(1 - k, g), kall[g, k], vall[g, k], scale, second(g))
 
     def nearer(g):
-        return attend(qc[g], all_of(kall, g), all_of(vall, g), scale)
-
-    def relay(g):
-        return remote(qd.at[g], qc.at[g], relay_send.at[g], qc_recv.at[g], mate)
+        return attend(flat(wc[window(at_c, g)]), all_of(kall, g), all_of(vall, g), scale)
+
+    def gather(ref, table, j, *lead):
+        return jnp.concatenate([ref[(*lead, table[0, j * per_block + b])] for b in range(per_block)], axis=0)
 
     def c_near(g):
         return (
@@ -250,110 +394,117 @@
             remote(td.at[g], sd.at[g], td_send.at[g], sd_recv.at[g], up),
         )
 
-    def start(copies):
-        for one in copies:
-            one.start()
-
-    @pl.when(jnp.logical_not(above))
-    def _():
-        qq[0] = jnp.zeros(qq.shape[1:], qq.dtype)
-
-    @pl.when(jnp.logical_not(feeds))
-    def _():
-        qc[...] = jnp.zeros(qc.shape, qc.dtype)
-
     pair = 2
     steps = groups // pair
 
-    def arrive_far(i):
-        @pl.when(above)
-        def _():
-            for u in range(pair):
-                g = i * pair + u
-                remote(q.at[g], qd.at[g], qd_send.at[g], qd_recv.at[g], partner).wait_recv()
-
-                @pl.when(even)
-                def _():
-                    relay(g).start()
+    def complete(p):
+        if p == steps - 1:
+            return chunks
+        return max(0, tokens * routed - capacity * (groups - pair * (p + 1))) // capacity
+
+    def pick(values, i):
+        out_ = jnp.int32(values[-1])
+        for at, value in enumerate(values[:-1]):
+            out_ = jnp.where(i == at, jnp.int32(value), out_)
+        return out_
+
+    ends = [complete(p) for p in range(steps)]
+    begins = [0] + ends[:-1]
+    comes = [min(pair * p, chunks) for p in range(steps + 1)]
 
     def arrive_near(i):
         @pl.when(feeds)
         def _():
-            for u in range(pair):
-                g = i * pair + u
-                remote(q.at[g], qc.at[g], qn_send.at[g], qc_recv.at[g], partner).wait_recv()
-
-    def send_far(i):
+            def one(j):
+                for h in range(halves):
+                    remote(
+                        qc.at[j, part_of(h)], qc.at[j, part_of(h)], qn_send.at[j, h], qc_recv.at[j, h], partner
+                    ).wait_recv()
+                wc[rows_of(j)] = qc[j]
+
+            each(pick(comes[:-1], i), pick(comes[1:], i), one)
+
+    loose = (chunks - 1) // pair - 1
+
+    def far_results(i):
         @pl.when(jnp.logical_and(odd, above))
         def _():
-            for u in range(pair):
-                g = i * pair + u
-                od[g] = op[0, g].astype(jnp.bfloat16)
-                td[g] = squeeze(lp[0, g], padded)
-
-    def release(upto_far, upto_near, from_far=0, from_near=0):
-        def go(make, a, b):
-            def body(g, carry):
-                start(make(g))
-                return carry
-
-            lax.fori_loop(a * pair, b * pair, body, 0)
-
-        @pl.when(jnp.logical_and(odd, above))
-        def _():
-            go(d_copies, from_far, upto_far)
-
-        @pl.when(even)
-        def _():
-            go(c_near, from_near, upto_near)
-
-    def send_relay(i):
-        @pl.when(jnp.logical_and(odd, feeds))
-        def _():
-            for u in range(pair):
-                start(c_relay(i * pair + u))
-
-    def block(far, near):
+            def one(j):
+                od[j] = gather(op, at_d, j, 0).astype(jnp.bfloat16)
+                td[j] = squeeze(gather(lp, at_d, j, 0), padded)
+
+                @pl.when(i >= loose)
+                def _():
+                    start(d_copies(j))
+
+            each(pick(begins, i), pick(ends, i), one)
+
+    def near_results(i, free):
+        def one(j):
+            oc[j] = gather(cp, at_c, j)
+            tc[j] = squeeze(gather(lc, at_c, j), padded)
+
+            @pl.when(odd)
+            def _():
+                @pl.when(feeds)
+                def _():
+                    start(c_relay(j))
+
+            @pl.when(jnp.logical_and(even, free))
+            def _():
+                start(c_near(j))
+
+        each(pick(begins, i), pick(ends, i), one)
+
+    def block_far(i):
         got = []
-        if far is not None:
-            for u in range(pair):
-                g = far * pair + u
-                got.append((k, g, both_shards(g)))
-                got.append((1 - k, g, one_shard(g)))
-        close = []
-        if near is not None:
-            for u in range(pair):
-                close.append((near * pair + u, nearer(near * pair + u)))
+        for u in range(pair):
+            g = i * pair + u
+            got.append((k, g, both_shards(g)))
+            got.append((1 - k, g, one_shard(g)))
         for at, g, (o, lse) in got:
-            op[at, g] = o
-            lp[at, g] = lse
-        for g, (o, lse) in close:
-            oc[g] = o.astype(jnp.bfloat16)
-            tc[g] = squeeze(lse, padded)
-
-    arrive_far(0)
-    block(0, None)
-    send_far(0)
+            op[at, rows_of(g)] = split(o)
+            lp[at, rows_of(g)] = split(lse)
+
+    def block_near(i):
+        got = [(i * pair + u, nearer(i * pair + u)) for u in range(pair)]
+        for g, (o, lse) in got:
+            cp[rows_of(g)] = split(o.astype(jnp.bfloat16))
+            lc[rows_of(g)] = split(lse)
+
+    @pl.when(feeds)
+    def _():
+        remote(tab, tab_c, tab_near.at[0], tab_near.at[1], partner).wait_recv()
+
+    @pl.when(jnp.logical_not(feeds))
+    def _():
+        tab_c[...] = tab[...]
+
+    local[2].start()
+    local[2].wait()
 
     def step(i, carry):
-        arrive_far(i)
-
-        @pl.when(i == steps - 1)
-        def _():
-            release(steps - 1, steps - 2)
-
-        arrive_near(i - 1)
-        block(i, i - 1)
-        send_far(i)
-        send_relay(i - 1)
+        block_far(i)
+        far_chunk(pair * i + pair)
+
+        @pl.when(i == loose)
+        def _():
+            @pl.when(jnp.logical_and(odd, above))
+            def _():
+                each(0, ends[loose - 1], lambda j: start(d_copies(j)))
+
+            @pl.when(jnp.logical_and(even, above))
+            def _():
+                each(0, ends[loose - 1], lambda j: start(c_near(j)))
+
+        arrive_near(i)
+        block_near(i)
+        near_results(i, jnp.logical_or(i >= loose, jnp.logical_not(above)))
+        far_chunk(pair * i + pair + 1)
+        far_results(i)
         return carry
 
-    lax.fori_loop(1, steps, step, 0)
-    release(steps, steps - 1, steps - 1, steps - 2)
-    arrive_near(steps - 1)
-    block(None, steps - 1)
-    release(steps, steps, steps, steps - 1)
-    send_relay(steps - 1)
+    lax.fori_loop(0, steps, step, 0)
 
     for i in range(2):
         kv_copy(i).wait_send()
@@ -366,38 +517,42 @@
                     one.wait_send()
                 return carry
 
-            lax.fori_loop(0, groups, body, 0)
-
-    sent(below, lambda g: (query_down(g),))
-    sent(odd, lambda g: (query_near(g),))
-    sent(jnp.logical_and(even, above), lambda g: (relay(g),))
+            lax.fori_loop(0, chunks, body, 0)
+
+    sent(below, query_down)
+    sent(odd, query_near)
+    sent(jnp.logical_and(even, above), relay)
+
+    @pl.when(below)
+    def _():
+        table_down().wait_send()
+
+    @pl.when(odd)
+    def _():
+        table_near().wait_send()
 
     @pl.when(jnp.logical_and(even, above))
     def _():
-        def join(g, carry):
+        table_relay().wait_send()
+
+    def join(g):
+        @pl.when(jnp.logical_and(jnp.logical_and(even, above), g < chunks))
+        def _():
             remote(oc.at[g], rx.at[g], oc_send.at[g], rx_recv.at[g], partner).wait_recv()
             remote(tc.at[g], sx.at[g], tc_send.at[g], sx_recv.at[g], partner).wait_recv()
-            o, lse = merge([(op[0, g], lp[0, g]), (rx[g], widen(sx[g], capacity))])
+            mine = (gather(op, at_d, g, 0), gather(lp, at_d, g, 0))
+            o, lse = merge([mine, (rx[g], widen(sx[g], capacity))])
             od[g] = o.astype(jnp.bfloat16)
             td[g] = squeeze(lse, padded)
             start(d_copies(g))
-            return carry
-
-        lax.fori_loop(0, groups, join, 0)
-
-    def absent(o, t):
-        o[...] = jnp.zeros(o.shape, o.dtype)
-        t[...] = jnp.full(t.shape, LOW, t.dtype)
-
-    @pl.when(even)
-    def _():
-        absent(rc, sc)
-
-    @pl.when(jnp.logical_not(below))
-    def _():
-        absent(rd, sd)
+
+    ahead = 2
+    for g in range(ahead):
+        join(jnp.int32(g))
 
     def finish(g, carry):
+        join(g + ahead)
+
         @pl.when(odd)
         def _():
             remote(oc.at[g], rc.at[g], oc_send.at[g], rc_recv.at[g], partner).wait_recv()
@@ -409,21 +564,26 @@
             remote(td.at[g], sd.at[g], td_send.at[g], sd_recv.at[g], partner).wait_recv()
 
         parts = [
-            (op[1, g], lp[1, g]), (rc[g], widen(sc[g], capacity)), (rd[g], widen(sd[g], capacity))
+            (gather(op, at_own, g, 1), gather(lp, at_own, g, 1)),
+            (rc[g], widen(sc[g], capacity)),
+            (rd[g], widen(sd[g], capacity)),
         ]
-        fin[pl.ds(pl.multiple_of(g * capacity, 16), capacity), :] = merge(parts)[0].astype(jnp.bfloat16)
+        fin[pl.ds(pl.multiple_of(g * capacity, BLOCK), capacity), :] = merge(parts)[0].astype(jnp.bfloat16)
         return carry
 
     sent(jnp.logical_and(odd, feeds), c_relay)
 
     tile = 256
-    tiles = groups * capacity // tile
+    tiles = fin.shape[0] // tile
+    fin[pl.ds(chunks * capacity, tiles * tile - chunks * capacity), :] = jnp.zeros(
+        (tiles * tile - chunks * capacity, width), fin.dtype
+    )
     lane = lax.broadcasted_iota(jnp.int32, (tokens, tile), 1).astype(jnp.float32)
     done = 0
-    stops = [2, 4, 6, 7, 8] if groups == 8 else [groups]
+    stops = [*range(2, chunks, 2), chunks]
     for s, stop in enumerate(stops):
         lax.fori_loop(stops[s - 1] if s else 0, stop, finish, 0)
-        last = stop == groups
+        last = stop == chunks
         upto = tiles if last else stop * capacity // tile
         for r in range(routed):
             slot = jnp.broadcast_to(slots[:, r : r + 1], (tokens, tile))
@@ -452,14 +612,17 @@
     context, groups, _ = keys.shape
     capacity = HEADS // groups * MOST
     padded = -(-capacity // LANES) * LANES
+    count = -(-(tokens * routed + groups * BLOCK) // capacity)
+    cut = (groups * capacity // BLOCK, BLOCK, width)
     vmem = pl.BlockSpec(memory_space=pltpu.VMEM)
     hbm = pl.BlockSpec(memory_space=pltpu.HBM)
     bf = lambda *shape: pltpu.VMEM(shape, jnp.bfloat16)
     f32 = lambda *shape: pltpu.VMEM(shape, jnp.float32)
     sem = lambda *shape: pltpu.SemaphoreType.DMA(shape)
-    chunks = lambda: bf(groups, capacity, width)
-    stats = lambda: f32(groups, 1, padded)
-    full = lambda: f32(groups, capacity, width)
+    table = lambda: pltpu.VMEM((1, 2 * TABLE), jnp.int32)
+    scalars = lambda: pltpu.SMEM((1, 2 * TABLE), jnp.int32)
+    chunks = lambda: bf(count, capacity, width)
+    stats = lambda: f32(count, 1, padded)
     return pl.pallas_call(
         functools.partial(kernel, n),
         out_shape=jax.ShapeDtypeStruct((tokens, routed, width), jnp.bfloat16),
@@ -468,13 +631,16 @@
         scratch_shapes=[
             bf(tokens, routed, width), pltpu.VMEM((routed, tokens), jnp.int32),
             bf(2, context, groups, width), f32(max(tokens * routed, LANES * groups), width), bf(routed * tokens, 2 * width),
-            f32(routed, tokens), f32(tokens, LANES), bf(2, groups, capacity, width), full(),
+            f32(routed, tokens), f32(tokens, LANES), bf(2, *cut), bf(*cut), f32(*cut),
             bf(groups, 2, context, width), bf(groups, 2, context, width),
-            chunks(), f32(2, groups, capacity, width), f32(2, groups, capacity, width),
+            table(), table(), table(), scalars(), scalars(), scalars(),
+            bf(count, capacity // BLOCK, BLOCK, width), bf(count, capacity // BLOCK, BLOCK, width),
+            f32(2, *cut), f32(2, *cut), bf(*cut), f32(*cut),
             chunks(), stats(), chunks(), stats(),
             chunks(), stats(), chunks(), stats(), chunks(), stats(),
-            bf(groups * capacity, width), f32(routed, tokens, width),
-        ] + [sem(2)] * 4 + [sem(groups)] * 15,
+            bf(-(-count * capacity // 256) * 256, width), f32(routed, tokens, width),
+        ] + [sem(2), sem(3), sem(2), sem(2), sem(1)] + [sem(2)] * 3
+        + [sem(count, 2)] * 5 + [sem(count)] * 10,
         compiler_params=pltpu.CompilerParams(
             collective_id=0, has_side_effects=True, vmem_limit_bytes=48 * 1024 * 1024
         ),

time: 45 us -> 43 us (0.956)
  Pallas kernels: 44 us -> 41.7 us
    pallas_call x1, Pallas kernels: 44 us -> 41.7 us  [shards(): pl.pallas_call(functools.partial(kernel, n), out_shape=jax.ShapeDtypeStru...]
where the time goes in v5:
time: 43 us; the launch traced here: 42.5 us
  Pallas kernels  41.7 us (97%)
  local copies, waits for them, and re-layouts  0.8 us (2%)
    pallas_call x1, Pallas kernels, shards(): pl.pallas_call(functools.partial(kernel, n), out_shape=jax.ShapeDtypeStru...  41.7 us

profile of v5, /device:TPU:8, one launch (start us, length us, event | category | flops | bytes accessed | tf_op | source)
XLA Modules:
  0.0 42.5 jit_solution(1546035771902810419)
XLA Ops:
  0.0 41.7 %fused.1 = bf16[256,8,128]{2,1,0:T(8,128)(2,1)S(1)} custom-call(bf16[256,8,128]{2,1,0:T(8,128)(2,1)} %q_hbm.1, s32[8,256]{1,0:T(8,128)} %bitcast.1, bf16[512,8,128]{2,1,0:T(8,128)(2,1)} %k_hbm.1, bf16[512,8,128]{2,1,0:T(8,128)(2,1)} %v_hbm.1), custom_call_target="tpu_custom_call" | custom-call | tf_op jit(solution)/shard_map/fused/pallas_call | solution.py:626
  41.7 0.8 %copy.6 = bf16[256,8,128]{2,1,0:T(8,128)(2,1)} copy(bf16[256,8,128]{2,1,0:T(8,128)(2,1)S(1)} %fused.1) | data formatting | bytes 1048576

commit v6 on v5

--- a/solution.py
+++ b/solution.py
@@ -181,18 +181,18 @@
 
     def query_down(j):
         return [
-            remote(query_part(j, h), qd.at[j, part_of(h)], qd_send.at[j, h], qd_recv.at[j, h], down)
+            remote(query_part(j, h), qd.at[j, part_of(h)], qd_send.at[0], qd_recv.at[j, h], down)
             for h in range(halves)
         ]
 
     def query_near(j):
         return [
-            remote(query_part(j, h), qc.at[j, part_of(h)], qn_send.at[j, h], qc_recv.at[j, h], mate)
+            remote(query_part(j, h), qc.at[j, part_of(h)], qn_send.at[0], qc_recv.at[j, h], mate)
             for h in range(halves)
         ]
 
     def relay_part(j, h):
-        return remote(qd.at[j, part_of(h)], qc.at[j, part_of(h)], relay_send.at[j, h], qc_recv.at[j, h], mate)
+        return remote(qd.at[j, part_of(h)], qc.at[j, part_of(h)], relay_send.at[0], qc_recv.at[j, h], mate)
 
     def relay(j):
         return [relay_part(j, h) for h in range(halves)]
@@ -243,7 +243,34 @@
 
         return carry
 
-    lax.fori_loop(0, chunks, pack, 0)
+    soon = min(3, chunks)
+    lax.fori_loop(0, soon, pack, 0)
+
+    part = 128
+
+    def turn(i, to):
+        def body(s, carry):
+            at = pl.multiple_of(s * part, part)
+            wide[pl.ds(0, part * groups), :] = raw[i, pl.ds(at, part)].astype(jnp.float32).reshape(part * groups, width)
+            for g in range(groups):
+                to[g, k, pl.ds(at, part), :] = wide[pl.ds(g, part, stride=groups), :].astype(jnp.bfloat16)
+            return carry
+
+        lax.fori_loop(0, context // part, body, 0)
+
+    def kv_copy(i):
+        a = (kall, vall)[i]
+        return remote(a.at[:, k], a.at[:, k], kv_send.at[i], kv_recv.at[i], partner)
+
+    def kv_arrival(i):
+        a = (kall, vall)[i]
+        return remote(a.at[:, 1 - k], a.at[:, 1 - k], kv_send.at[i], kv_recv.at[i], partner)
+
+    for i, to in enumerate((kall, vall)):
+        raws[i].wait()
+        turn(i, to)
+        kv_copy(i).start()
+    lax.fori_loop(soon, chunks, pack, 0)
 
     local = [
         pltpu.make_async_copy(a, b, tab_sem.at[i])
@@ -253,8 +280,16 @@
     rest = (groups - chunks) * per_block
     wq[1, pl.ds(chunks * per_block, rest)] = jnp.zeros((rest, BLOCK, width), wq.dtype)
     pos[pl.ds(chunks * per_block, rest)] = jnp.zeros((rest, BLOCK, width), pos.dtype)
-    wq[0] = jnp.zeros(wq.shape[1:], wq.dtype)
-    wc[...] = jnp.zeros(wc.shape, wc.dtype)
+    wq[0, pl.ds(chunks * per_block, rest)] = jnp.zeros((rest, BLOCK, width), wq.dtype)
+    wc[pl.ds(chunks * per_block, rest)] = jnp.zeros((rest, BLOCK, width), wc.dtype)
+
+    @pl.when(jnp.logical_not(above))
+    def _():
+        wq[0] = jnp.zeros(wq.shape[1:], wq.dtype)
+
+    @pl.when(jnp.logical_not(feeds))
+    def _():
+        wc[...] = jnp.zeros(wc.shape, wc.dtype)
 
     def each(a, b, body):
         def go(j, carry):
@@ -279,24 +314,12 @@
     local[0].wait()
     local[1].wait()
 
-    def absent(o, t):
-        o[...] = jnp.zeros(o.shape, o.dtype)
-        t[...] = jnp.full(t.shape, LOW, t.dtype)
-
-    @pl.when(even)
-    def _():
-        absent(rc, sc)
-
-    @pl.when(jnp.logical_not(below))
-    def _():
-        absent(rd, sd)
-
     def far_chunk(j):
         @pl.when(jnp.logical_and(above, j < chunks))
         def _():
             for h in range(halves):
                 remote(
-                    qd.at[j, part_of(h)], qd.at[j, part_of(h)], qd_send.at[j, h], qd_recv.at[j, h], partner
+                    qd.at[j, part_of(h)], qd.at[j, part_of(h)], qd_send.at[0], qd_recv.at[j, h], partner
                 ).wait_recv()
 
                 @pl.when(even)
@@ -307,30 +330,6 @@
 
     far_chunk(jnp.int32(0))
 
-    part = 128
-
-    def turn(i, to):
-        def body(s, carry):
-            at = pl.multiple_of(s * part, part)
-            wide[pl.ds(0, part * groups), :] = raw[i, pl.ds(at, part)].astype(jnp.float32).reshape(part * groups, width)
-            for g in range(groups):
-                to[g, k, pl.ds(at, part), :] = wide[pl.ds(g, part, stride=groups), :].astype(jnp.bfloat16)
-            return carry
-
-        lax.fori_loop(0, context // part, body, 0)
-
-    def kv_copy(i):
-        a = (kall, vall)[i]
-        return remote(a.at[:, k], a.at[:, k], kv_send.at[i], kv_recv.at[i], partner)
-
-    def kv_arrival(i):
-        a = (kall, vall)[i]
-        return remote(a.at[:, 1 - k], a.at[:, 1 - k], kv_send.at[i], kv_recv.at[i], partner)
-
-    for i, to in enumerate((kall, vall)):
-        raws[i].wait()
-        turn(i, to)
-        kv_copy(i).start()
     far_chunk(jnp.int32(1))
     for i in range(2):
         kv_arrival(i).wait_recv()
@@ -378,20 +377,20 @@
 
     def c_near(g):
         return (
-            remote(oc.at[g], rc.at[g], oc_send.at[g], rc_recv.at[g], mate),
-            remote(tc.at[g], sc.at[g], tc_send.at[g], sc_recv.at[g], mate),
+            remote(oc.at[g], rc.at[g], oc_send.at[0], rc_recv.at[g], mate),
+            remote(tc.at[g], sc.at[g], tc_send.at[0], sc_recv.at[g], mate),
         )
 
     def c_relay(g):
         return (
-            remote(oc.at[g], rx.at[g], oc_send.at[g], rx_recv.at[g], mate),
-            remote(tc.at[g], sx.at[g], tc_send.at[g], sx_recv.at[g], mate),
+            remote(oc.at[g], rx.at[g], oc_send.at[0], rx_recv.at[g], mate),
+            remote(tc.at[g], sx.at[g], tc_send.at[0], sx_recv.at[g], mate),
         )
 
     def d_copies(g):
         return (
-            remote(od.at[g], rd.at[g], od_send.at[g], rd_recv.at[g], up),
-            remote(td.at[g], sd.at[g], td_send.at[g], sd_recv.at[g], up),
+            remote(od.at[g], rd.at[g], od_send.at[0], rd_recv.at[g], up),
+            remote(td.at[g], sd.at[g], td_send.at[0], sd_recv.at[g], up),
         )
 
     pair = 2
@@ -418,7 +417,7 @@
             def one(j):
                 for h in range(halves):
                     remote(
-                        qc.at[j, part_of(h)], qc.at[j, part_of(h)], qn_send.at[j, h], qc_recv.at[j, h], partner
+                        qc.at[j, part_of(h)], qc.at[j, part_of(h)], qn_send.at[0], qc_recv.at[j, h], partner
                     ).wait_recv()
                 wc[rows_of(j)] = qc[j]
 
@@ -509,19 +508,15 @@
     for i in range(2):
         kv_copy(i).wait_send()
 
-    def sent(there, make):
+    def sent(there, *flows):
         @pl.when(there)
         def _():
-            def body(g, carry):
-                for one in make(g):
-                    one.wait_send()
-                return carry
-
-            lax.fori_loop(0, chunks, body, 0)
-
-    sent(below, query_down)
-    sent(odd, query_near)
-    sent(jnp.logical_and(even, above), relay)
+            for ref, sem in flows:
+                remote(ref, ref, sem.at[0], sem.at[0], partner).wait_send()
+
+    sent(below, (qd, qd_send))
+    sent(odd, (qd, qn_send))
+    sent(jnp.logical_and(even, above), (qd, relay_send))
 
     @pl.when(below)
     def _():
@@ -538,15 +533,27 @@
     def join(g):
         @pl.when(jnp.logical_and(jnp.logical_and(even, above), g < chunks))
         def _():
-            remote(oc.at[g], rx.at[g], oc_send.at[g], rx_recv.at[g], partner).wait_recv()
-            remote(tc.at[g], sx.at[g], tc_send.at[g], sx_recv.at[g], partner).wait_recv()
+            remote(oc.at[g], rx.at[g], oc_send.at[0], rx_recv.at[g], partner).wait_recv()
+            remote(tc.at[g], sx.at[g], tc_send.at[0], sx_recv.at[g], partner).wait_recv()
             mine = (gather(op, at_d, g, 0), gather(lp, at_d, g, 0))
             o, lse = merge([mine, (rx[g], widen(sx[g], capacity))])
             od[g] = o.astype(jnp.bfloat16)
             td[g] = squeeze(lse, padded)
             start(d_copies(g))
 
-    ahead = 2
+    def absent(o, t):
+        o[...] = jnp.zeros(o.shape, o.dtype)
+        t[...] = jnp.full(t.shape, LOW, t.dtype)
+
+    @pl.when(even)
+    def _():
+        absent(rc, sc)
+
+    @pl.when(jnp.logical_not(below))
+    def _():
+        absent(rd, sd)
+
+    ahead = 4
     for g in range(ahead):
         join(jnp.int32(g))
 
@@ -555,13 +562,13 @@
 
         @pl.when(odd)
         def _():
-            remote(oc.at[g], rc.at[g], oc_send.at[g], rc_recv.at[g], partner).wait_recv()
-            remote(tc.at[g], sc.at[g], tc_send.at[g], sc_recv.at[g], partner).wait_recv()
+            remote(oc.at[g], rc.at[g], oc_send.at[0], rc_recv.at[g], partner).wait_recv()
+            remote(tc.at[g], sc.at[g], tc_send.at[0], sc_recv.at[g], partner).wait_recv()
 
         @pl.when(below)
         def _():
-            remote(od.at[g], rd.at[g], od_send.at[g], rd_recv.at[g], partner).wait_recv()
-            remote(td.at[g], sd.at[g], td_send.at[g], sd_recv.at[g], partner).wait_recv()
+            remote(od.at[g], rd.at[g], od_send.at[0], rd_recv.at[g], partner).wait_recv()
+            remote(td.at[g], sd.at[g], td_send.at[0], sd_recv.at[g], partner).wait_recv()
 
         parts = [
             (gather(op, at_own, g, 1), gather(lp, at_own, g, 1)),
@@ -571,7 +578,7 @@
         fin[pl.ds(pl.multiple_of(g * capacity, BLOCK), capacity), :] = merge(parts)[0].astype(jnp.bfloat16)
         return carry
 
-    sent(jnp.logical_and(odd, feeds), c_relay)
+    sent(jnp.logical_and(odd, feeds), (oc, oc_send), (tc, tc_send))
 
     tile = 256
     tiles = fin.shape[0] // tile
@@ -603,8 +610,8 @@
         done = upto
     out[...] = wide[pl.ds(0, tokens * routed), :].reshape(tokens, routed, width).astype(jnp.bfloat16)
 
-    sent(above, d_copies)
-    sent(even, c_near)
+    sent(above, (od, od_send), (td, td_send))
+    sent(even, (oc, oc_send), (tc, tc_send))
 
 
 def shards(n, queries, keys, values, routes):
@@ -640,7 +647,7 @@
             chunks(), stats(), chunks(), stats(), chunks(), stats(),
             bf(-(-count * capacity // 256) * 256, width), f32(routed, tokens, width),
         ] + [sem(2), sem(3), sem(2), sem(2), sem(1)] + [sem(2)] * 3
-        + [sem(count, 2)] * 5 + [sem(count)] * 10,
+        + [sem(1)] * 2 + [sem(count, 2)] * 2 + [sem(1)] * 5 + [sem(count)] * 6,
         compiler_params=pltpu.CompilerParams(
             collective_id=0, has_side_effects=True, vmem_limit_bytes=48 * 1024 * 1024
         ),

time: 43 us -> 39.5 us (0.919)
  Pallas kernels: 41.7 us -> 38.5 us
    pallas_call x1, Pallas kernels: 41.7 us -> 38.5 us  [shards(): pl.pallas_call(functools.partial(kernel, n), out_shape=jax.ShapeDtypeStru...]
where the time goes in v6:
time: 39.5 us; the launch traced here: 39.3 us
  Pallas kernels  38.5 us (97%)
  local copies, waits for them, and re-layouts  0.8 us (2%)
    pallas_call x1, Pallas kernels, shards(): pl.pallas_call(functools.partial(kernel, n), out_shape=jax.ShapeDtypeStru...  38.5 us
    unnamed x1, local copies, waits for them, and re-layouts  0.8 us

profile of v6, /device:TPU:8, one launch (start us, length us, event | category | flops | bytes accessed | tf_op | source)
XLA Modules:
  0.0 39.3 jit_solution(10109333056423633439)
XLA Ops:
  0.0 38.5 %fused.1 = bf16[256,8,128]{2,1,0:T(8,128)(2,1)S(1)} custom-call(bf16[256,8,128]{2,1,0:T(8,128)(2,1)} %q_hbm.1, s32[8,256]{1,0:T(8,128)} %bitcast.1, bf16[512,8,128]{2,1,0:T(8,128)(2,1)} %k_hbm.1, bf16[512,8,128]{2,1,0:T(8,128)(2,1)} %v_hbm.1), custom_call_target="tpu_custom_call" | custom-call | tf_op jit(solution)/shard_map/fused/pallas_call | solution.py:633
  38.5 0.8 %copy.6 = bf16[256,8,128]{2,1,0:T(8,128)(2,1)} copy(bf16[256,8,128]{2,1,0:T(8,128)(2,1)S(1)} %fused.1) | data formatting | bytes 1048576

commit v7 on v6

--- a/solution.py
+++ b/solution.py
@@ -482,54 +482,6 @@
     local[2].start()
     local[2].wait()
 
-    def step(i, carry):
-        block_far(i)
-        far_chunk(pair * i + pair)
-
-        @pl.when(i == loose)
-        def _():
-            @pl.when(jnp.logical_and(odd, above))
-            def _():
-                each(0, ends[loose - 1], lambda j: start(d_copies(j)))
-
-            @pl.when(jnp.logical_and(even, above))
-            def _():
-                each(0, ends[loose - 1], lambda j: start(c_near(j)))
-
-        arrive_near(i)
-        block_near(i)
-        near_results(i, jnp.logical_or(i >= loose, jnp.logical_not(above)))
-        far_chunk(pair * i + pair + 1)
-        far_results(i)
-        return carry
-
-    lax.fori_loop(0, steps, step, 0)
-
-    for i in range(2):
-        kv_copy(i).wait_send()
-
-    def sent(there, *flows):
-        @pl.when(there)
-        def _():
-            for ref, sem in flows:
-                remote(ref, ref, sem.at[0], sem.at[0], partner).wait_send()
-
-    sent(below, (qd, qd_send))
-    sent(odd, (qd, qn_send))
-    sent(jnp.logical_and(even, above), (qd, relay_send))
-
-    @pl.when(below)
-    def _():
-        table_down().wait_send()
-
-    @pl.when(odd)
-    def _():
-        table_near().wait_send()
-
-    @pl.when(jnp.logical_and(even, above))
-    def _():
-        table_relay().wait_send()
-
     def join(g):
         @pl.when(jnp.logical_and(jnp.logical_and(even, above), g < chunks))
         def _():
@@ -541,6 +493,58 @@
             td[g] = squeeze(lse, padded)
             start(d_copies(g))
 
+    def step(i, carry):
+        block_far(i)
+        far_chunk(pair * i + pair)
+
+        @pl.when(i == loose)
+        def _():
+            @pl.when(jnp.logical_and(odd, above))
+            def _():
+                each(0, ends[loose - 1], lambda j: start(d_copies(j)))
+
+            @pl.when(jnp.logical_and(even, above))
+            def _():
+                each(0, ends[loose - 1], lambda j: start(c_near(j)))
+
+        @pl.when(i == steps - 1)
+        def _():
+            join(jnp.int32(0))
+
+        arrive_near(i)
+        block_near(i)
+        near_results(i, jnp.logical_or(i >= loose, jnp.logical_not(above)))
+        far_chunk(pair * i + pair + 1)
+        far_results(i)
+        return carry
+
+    lax.fori_loop(0, steps, step, 0)
+
+    for i in range(2):
+        kv_copy(i).wait_send()
+
+    def sent(there, *flows):
+        @pl.when(there)
+        def _():
+            for ref, sem in flows:
+                remote(ref, ref, sem.at[0], sem.at[0], partner).wait_send()
+
+    sent(below, (qd, qd_send))
+    sent(odd, (qd, qn_send))
+    sent(jnp.logical_and(even, above), (qd, relay_send))
+
+    @pl.when(below)
+    def _():
+        table_down().wait_send()
+
+    @pl.when(odd)
+    def _():
+        table_near().wait_send()
+
+    @pl.when(jnp.logical_and(even, above))
+    def _():
+        table_relay().wait_send()
+
     def absent(o, t):
         o[...] = jnp.zeros(o.shape, o.dtype)
         t[...] = jnp.full(t.shape, LOW, t.dtype)
@@ -553,8 +557,8 @@
     def _():
         absent(rd, sd)
 
-    ahead = 4
-    for g in range(ahead):
+    ahead = 3
+    for g in range(1, ahead):
         join(jnp.int32(g))
 
     def finish(g, carry):

time: 39.5 us -> 38.9 us (0.985)
  Pallas kernels: 38.5 us -> 37.9 us
    pallas_call x1, Pallas kernels: 38.5 us -> 37.9 us  [shards(): pl.pallas_call(functools.partial(kernel, n), out_shape=jax.ShapeDtypeStru...]
where the time goes in v7:
time: 38.9 us; the launch traced here: 38.7 us
  Pallas kernels  37.9 us (97%)
  local copies, waits for them, and re-layouts  0.8 us (2%)
    pallas_call x1, Pallas kernels, shards(): pl.pallas_call(functools.partial(kernel, n), out_shape=jax.ShapeDtypeStru...  37.9 us
    unnamed x1, local copies, waits for them, and re-layouts  0.8 us

profile of v7, /device:TPU:8, one launch (start us, length us, event | category | flops | bytes accessed | tf_op | source)
XLA Modules:
  0.0 38.7 jit_solution(5490636949399358116)
XLA Ops:
  0.0 37.9 %fused.1 = bf16[256,8,128]{2,1,0:T(8,128)(2,1)S(1)} custom-call(bf16[256,8,128]{2,1,0:T(8,128)(2,1)} %q_hbm.1, s32[8,256]{1,0:T(8,128)} %bitcast.1, bf16[512,8,128]{2,1,0:T(8,128)(2,1)} %k_hbm.1, bf16[512,8,128]{2,1,0:T(8,128)(2,1)} %v_hbm.1), custom_call_target="tpu_custom_call" | custom-call | tf_op jit(solution)/shard_map/fused/pallas_call | solution.py:637
  37.9 0.8 %copy.6 = bf16[256,8,128]{2,1,0:T(8,128)(2,1)} copy(bf16[256,8,128]{2,1,0:T(8,128)(2,1)S(1)} %fused.1) | data formatting | bytes 1048576

commit v8 on v7

--- a/solution.py
+++ b/solution.py
@@ -114,7 +114,7 @@
         for i, (a, b) in enumerate(((routes_hbm, routes_t), (q_hbm, q_in)))
     ]
     raws = [pltpu.make_async_copy(a, raw.at[i], raw_sem.at[i]) for i, a in enumerate((k_hbm, v_hbm))]
-    for one in ins + raws:
+    for one in ins:
         one.start()
     ins[0].wait()
 
@@ -153,13 +153,14 @@
     slots[...] = jnp.concatenate([slot_all] * (LANES // routed), axis=0).T
 
     ins[1].wait()
+    for one in raws:
+        one.start()
     wide[pl.ds(0, tokens * routed), :] = q_in[...].astype(jnp.float32).reshape(tokens * routed, width)
     token = lax.broadcasted_iota(jnp.int32, (tokens, width), 0).astype(jnp.float32).astype(jnp.bfloat16)
     for r in range(routed):
         rights[pl.ds(r * tokens, tokens), :width] = wide[pl.ds(r, tokens, stride=routed), :].astype(jnp.bfloat16)
         rights[pl.ds(r * tokens, tokens), width:] = token
 
-    pl.semaphore_wait(barrier, 2 + below.astype(jnp.int32) + above.astype(jnp.int32))
 
     def rows_of(j):
         return pl.ds(j * per_block, per_block)
@@ -210,17 +211,9 @@
     def table_relay():
         return remote(tab_d, tab_c, tab_relay.at[0], tab_near.at[1], mate)
 
-    @pl.when(below)
-    def _():
-        table_down().start()
-
-    @pl.when(odd)
-    def _():
-        table_near().start()
-
     place = lax.broadcasted_iota(jnp.int32, (capacity, tokens), 0).astype(jnp.float32)
 
-    def pack(g, carry):
+    def pack_rows(g):
         at = (g * capacity).astype(jnp.float32)
         here = jnp.concatenate(
             [
@@ -233,6 +226,7 @@
         wq[1, rows_of(g)] = split(both[:, :width].astype(jnp.bfloat16))
         pos[rows_of(g)] = split(both[:, width:])
 
+    def pack_send(g):
         @pl.when(below)
         def _():
             start(query_down(g))
@@ -241,10 +235,25 @@
         def _():
             start(query_near(g))
 
+    def pack(g, carry):
+        pack_rows(g)
+        pack_send(g)
         return carry
 
+    pack_rows(jnp.int32(0))
+    pl.semaphore_wait(barrier, 2 + below.astype(jnp.int32) + above.astype(jnp.int32))
+
+    @pl.when(below)
+    def _():
+        table_down().start()
+
+    @pl.when(odd)
+    def _():
+        table_near().start()
+
+    pack_send(jnp.int32(0))
     soon = min(3, chunks)
-    lax.fori_loop(0, soon, pack, 0)
+    lax.fori_loop(1, soon, pack, 0)
 
     part = 128
 

time: 38.9 us -> 38.4 us (0.987)
  Pallas kernels: 37.9 us -> 37.4 us
    pallas_call x1, Pallas kernels: 37.9 us -> 37.4 us  [shards(): pl.pallas_call(functools.partial(kernel, n), out_shape=jax.ShapeDtypeStru...]
where the time goes in v8:
time: 38.4 us; the launch traced here: 38.3 us
  Pallas kernels  37.4 us (97%)
  local copies, waits for them, and re-layouts  0.8 us (2%)
    pallas_call x1, Pallas kernels, shards(): pl.pallas_call(functools.partial(kernel, n), out_shape=jax.ShapeDtypeStru...  37.4 us
    unnamed x1, local copies, waits for them, and re-layouts  0.8 us

profile of v8, /device:TPU:8, one launch (start us, length us, event | category | flops | bytes accessed | tf_op | source)
XLA Modules:
  0.0 38.3 jit_solution(16416273028920181745)
XLA Ops:
  0.0 37.4 %fused.1 = bf16[256,8,128]{2,1,0:T(8,128)(2,1)S(1)} custom-call(bf16[256,8,128]{2,1,0:T(8,128)(2,1)} %q_hbm.1, s32[8,256]{1,0:T(8,128)} %bitcast.1, bf16[512,8,128]{2,1,0:T(8,128)(2,1)} %k_hbm.1, bf16[512,8,128]{2,1,0:T(8,128)(2,1)} %v_hbm.1), custom_call_target="tpu_custom_call" | custom-call | tf_op jit(solution)/shard_map/fused/pallas_call | solution.py:646
  37.5 0.8 %copy.6 = bf16[256,8,128]{2,1,0:T(8,128)(2,1)} copy(bf16[256,8,128]{2,1,0:T(8,128)(2,1)S(1)} %fused.1) | data formatting | bytes 1048576

commit v9 on v8

--- a/solution.py
+++ b/solution.py
@@ -281,6 +281,12 @@
         kv_copy(i).start()
     lax.fori_loop(soon, chunks, pack, 0)
 
+    used = -(-tokens * routed // BLOCK) + groups
+    last_rows = (used - (chunks - 1) * per_block) * BLOCK
+
+    for to in (rx, rc, rd):
+        to[chunks - 1, last_rows:, :] = jnp.zeros((capacity - last_rows, width), to.dtype)
+
     local = [
         pltpu.make_async_copy(a, b, tab_sem.at[i])
         for i, (a, b) in enumerate(((tab_d, at_d), (tab, at_own), (tab_c, at_c)))
@@ -384,23 +390,37 @@
     def gather(ref, table, j, *lead):
         return jnp.concatenate([ref[(*lead, table[0, j * per_block + b])] for b in range(per_block)], axis=0)
 
-    def c_near(g):
-        return (
-            remote(oc.at[g], rc.at[g], oc_send.at[0], rc_recv.at[g], mate),
-            remote(tc.at[g], sc.at[g], tc_send.at[0], sc_recv.at[g], mate),
-        )
-
-    def c_relay(g):
-        return (
-            remote(oc.at[g], rx.at[g], oc_send.at[0], rx_recv.at[g], mate),
-            remote(tc.at[g], sx.at[g], tc_send.at[0], sx_recv.at[g], mate),
-        )
-
-    def d_copies(g):
-        return (
-            remote(od.at[g], rd.at[g], od_send.at[0], rd_recv.at[g], up),
-            remote(td.at[g], sd.at[g], td_send.at[0], sd_recv.at[g], up),
-        )
+    def results(o_from, t_from, o_to, t_to, o_send, t_send, o_recv, t_recv, to):
+        def make(g, act):
+            def go(rows):
+                act(
+                    remote(
+                        o_from.at[g, pl.ds(0, rows)], o_to.at[g, pl.ds(0, rows)],
+                        o_send.at[0], o_recv.at[g], to,
+                    )
+                )
+
+            @pl.when(g < chunks - 1)
+            def _():
+                go(capacity)
+
+            @pl.when(g == chunks - 1)
+            def _():
+                go(last_rows)
+
+            act(remote(t_from.at[g], t_to.at[g], t_send.at[0], t_recv.at[g], to))
+
+        return make
+
+    c_near = results(oc, tc, rc, sc, oc_send, tc_send, rc_recv, sc_recv, mate)
+    c_relay = results(oc, tc, rx, sx, oc_send, tc_send, rx_recv, sx_recv, mate)
+    d_copies = results(od, td, rd, sd, od_send, td_send, rd_recv, sd_recv, up)
+
+    def begin(one):
+        one.start()
+
+    def arrived(one):
+        one.wait_recv()
 
     pair = 2
     steps = groups // pair
@@ -443,7 +463,7 @@
 
                 @pl.when(i >= loose)
                 def _():
-                    start(d_copies(j))
+                    d_copies(j, begin)
 
             each(pick(begins, i), pick(ends, i), one)
 
@@ -456,11 +476,11 @@
             def _():
                 @pl.when(feeds)
                 def _():
-                    start(c_relay(j))
+                    c_relay(j, begin)
 
             @pl.when(jnp.logical_and(even, free))
             def _():
-                start(c_near(j))
+                c_near(j, begin)
 
         each(pick(begins, i), pick(ends, i), one)
 
@@ -494,13 +514,12 @@
     def join(g):
         @pl.when(jnp.logical_and(jnp.logical_and(even, above), g < chunks))
         def _():
-            remote(oc.at[g], rx.at[g], oc_send.at[0], rx_recv.at[g], partner).wait_recv()
-            remote(tc.at[g], sx.at[g], tc_send.at[0], sx_recv.at[g], partner).wait_recv()
+            c_relay(g, arrived)
             mine = (gather(op, at_d, g, 0), gather(lp, at_d, g, 0))
             o, lse = merge([mine, (rx[g], widen(sx[g], capacity))])
             od[g] = o.astype(jnp.bfloat16)
             td[g] = squeeze(lse, padded)
-            start(d_copies(g))
+            d_copies(g, begin)
 
     def step(i, carry):
         block_far(i)
@@ -510,11 +529,11 @@
         def _():
             @pl.when(jnp.logical_and(odd, above))
             def _():
-                each(0, ends[loose - 1], lambda j: start(d_copies(j)))
+                each(0, ends[loose - 1], lambda j: d_copies(j, begin))
 
             @pl.when(jnp.logical_and(even, above))
             def _():
-                each(0, ends[loose - 1], lambda j: start(c_near(j)))
+                each(0, ends[loose - 1], lambda j: c_near(j, begin))
 
         @pl.when(i == steps - 1)
         def _():
@@ -532,6 +551,8 @@
     for i in range(2):
         kv_copy(i).wait_send()
 
+    spent = wq.at[1, pl.ds(0, used)]
+
     def sent(there, *flows):
         @pl.when(there)
         def _():
@@ -575,13 +596,11 @@
 
         @pl.when(odd)
         def _():
-            remote(oc.at[g], rc.at[g], oc_send.at[0], rc_recv.at[g], partner).wait_recv()
-            remote(tc.at[g], sc.at[g], tc_send.at[0], sc_recv.at[g], partner).wait_recv()
+            c_near(g, arrived)
 
         @pl.when(below)
         def _():
-            remote(od.at[g], rd.at[g], od_send.at[0], rd_recv.at[g], partner).wait_recv()
-            remote(td.at[g], sd.at[g], td_send.at[0], sd_recv.at[g], partner).wait_recv()
+            d_copies(g, arrived)
 
         parts = [
             (gather(op, at_own, g, 1), gather(lp, at_own, g, 1)),
@@ -591,7 +610,7 @@
         fin[pl.ds(pl.multiple_of(g * capacity, BLOCK), capacity), :] = merge(parts)[0].astype(jnp.bfloat16)
         return carry
 
-    sent(jnp.logical_and(odd, feeds), (oc, oc_send), (tc, tc_send))
+    sent(jnp.logical_and(odd, feeds), (spent, oc_send), (tc, tc_send))
 
     tile = 256
     tiles = fin.shape[0] // tile
@@ -623,8 +642,8 @@
         done = upto
     out[...] = wide[pl.ds(0, tokens * routed), :].reshape(tokens, routed, width).astype(jnp.bfloat16)
 
-    sent(above, (od, od_send), (td, td_send))
-    sent(even, (oc, oc_send), (tc, tc_send))
+    sent(above, (spent, od_send), (td, td_send))
+    sent(even, (spent, oc_send), (tc, tc_send))
 
 
 def shards(n, queries, keys, values, routes):

time: 38.4 us -> 38.3 us (level)
  no operation moved by 1% of the time
where the time goes in v9:
time: 38.3 us; the launch traced here: 38 us
  Pallas kernels  37.2 us (97%)
  local copies, waits for them, and re-layouts  0.8 us (2%)
    pallas_call x1, Pallas kernels, shards(): pl.pallas_call(functools.partial(kernel, n), out_shape=jax.ShapeDtypeStru...  37.2 us
    unnamed x1, local copies, waits for them, and re-layouts  0.8 us

profile of v9, /device:TPU:8, one launch (start us, length us, event | category | flops | bytes accessed | tf_op | source)
XLA Modules:
  0.0 38.0 jit_solution(17263085219868112815)
XLA Ops:
  0.0 37.2 %fused.1 = bf16[256,8,128]{2,1,0:T(8,128)(2,1)S(1)} custom-call(bf16[256,8,128]{2,1,0:T(8,128)(2,1)} %q_hbm.1, s32[8,256]{1,0:T(8,128)} %bitcast.1, bf16[512,8,128]{2,1,0:T(8,128)(2,1)} %k_hbm.1, bf16[512,8,128]{2,1,0:T(8,128)(2,1)} %v_hbm.1), custom_call_target="tpu_custom_call" | custom-call | tf_op jit(solution)/shard_map/fused/pallas_call | solution.py:665
  37.2 0.8 %copy.6 = bf16[256,8,128]{2,1,0:T(8,128)(2,1)} copy(bf16[256,8,128]{2,1,0:T(8,128)(2,1)S(1)} %fused.1) | data formatting | bytes 1048576

commit v10 on v9

--- a/solution.py
+++ b/solution.py
@@ -171,7 +171,7 @@
     def flat(x):
         return x.reshape(x.shape[0] * BLOCK, width)
 
-    halves = 2
+    halves = 4
     part_rows = per_block // halves
 
     def part_of(h):
@@ -679,7 +679,7 @@
             chunks(), stats(), chunks(), stats(), chunks(), stats(),
             bf(-(-count * capacity // 256) * 256, width), f32(routed, tokens, width),
         ] + [sem(2), sem(3), sem(2), sem(2), sem(1)] + [sem(2)] * 3
-        + [sem(1)] * 2 + [sem(count, 2)] * 2 + [sem(1)] * 5 + [sem(count)] * 6,
+        + [sem(1)] * 2 + [sem(count, 4)] * 2 + [sem(1)] * 5 + [sem(count)] * 6,
         compiler_params=pltpu.CompilerParams(
             collective_id=0, has_side_effects=True, vmem_limit_bytes=48 * 1024 * 1024
         ),

time: 38.3 us -> 38.6 us (level)
  Pallas kernels: 37.2 us -> 37.6 us
    pallas_call x1, Pallas kernels: 37.2 us -> 37.6 us  [shards(): pl.pallas_call(functools.partial(kernel, n), out_shape=jax.ShapeDtypeStru...]
where the time goes in v10:
time: 38.6 us; the launch traced here: 38.4 us
  Pallas kernels  37.6 us (97%)
  local copies, waits for them, and re-layouts  0.8 us (2%)
    pallas_call x1, Pallas kernels, shards(): pl.pallas_call(functools.partial(kernel, n), out_shape=jax.ShapeDtypeStru...  37.6 us
    unnamed x1, local copies, waits for them, and re-layouts  0.8 us

profile of v10, /device:TPU:8, one launch (start us, length us, event | category | flops | bytes accessed | tf_op | source)
XLA Modules:
  0.0 38.4 jit_solution(14065420299125468725)
XLA Ops:
  0.0 37.6 %fused.1 = bf16[256,8,128]{2,1,0:T(8,128)(2,1)S(1)} custom-call(bf16[256,8,128]{2,1,0:T(8,128)(2,1)} %q_hbm.1, s32[8,256]{1,0:T(8,128)} %bitcast.1, bf16[512,8,128]{2,1,0:T(8,128)(2,1)} %k_hbm.1, bf16[512,8,128]{2,1,0:T(8,128)(2,1)} %v_hbm.1), custom_call_target="tpu_custom_call" | custom-call | tf_op jit(solution)/shard_map/fused/pallas_call | solution.py:665
  37.6 0.8 %copy.6 = bf16[256,8,128]{2,1,0:T(8,128)(2,1)} copy(bf16[256,8,128]{2,1,0:T(8,128)(2,1)S(1)} %fused.1) | data formatting | bytes 1048576
